TPU v7x, 32 devices: a whole 2x2x4 slice. The times are simulated.
32 devices in a mesh: wide: 8 (over y, x, core), narrow: 4 (over z).
Axes of the slice: x: 2, y: 2, z: 4, core: 2. Of those that a mesh axis runs over, the one named last changes fastest.
Arguments:
- node_features: bfloat16 [2048, 25, 128], P(('wide', 'narrow')), may hold values from -6 to 6
- frames: bfloat16 [2048, 48, 165], P(('wide', 'narrow')), may hold values from -6 to 6
- radial: bfloat16 [2048, 48, 128], P(('wide', 'narrow')), may hold values from 0.29882812 to 3
- neighbours: int32 [2048, 48], P(('wide', 'narrow')), may hold values from 0 to 2047, as said below
- counts: int32 [2048], P(('wide', 'narrow')), may hold values from 16 to 48
- coefficients: float32 [32], P('wide'), may hold values from 0.05 to 0.5
- w_zero: bfloat16 [32, 640, 640], P('wide'), may hold values from -0.25 to 0.25
- w_one: bfloat16 [32, 2, 512, 512], P('wide'), may hold values from -0.1875 to 0.1875
- w_two: bfloat16 [32, 2, 384, 384], P('wide'), may hold values from -0.21875 to 0.21875
- w_three: bfloat16 [32, 2, 256, 256], P('wide'), may hold values from -0.25 to 0.25
- w_four: bfloat16 [32, 2, 128, 128], P('wide'), may hold values from -0.375 to 0.375
Outputs:
- conv_out: float32 [2048, 25, 128], P(('wide', 'narrow'))
Inputs may be any that keep to these rules, and one draw needn't show every extreme that they name: `neighbours`: each neighbour of an atom lies in the atom's own aligned block of 64 atoms or in one of the two cyclically adjacent blocks. `counts`: slots at or beyond an atom's count are padding and carry arbitrary indices.
All inputs are finite; a program needn't handle non-finite values.
Results may differ from a plain program's by a relative error of at most 0.02.
Values may be sent and summed in bfloat16 or wider, within the bound.
A program may use at most 192 MiB of HBM per device.

v0:
```python
import functools

import jax
import jax.numpy as jnp
import numpy as np
from jax import lax
from jax.experimental import pallas as pl
from jax.experimental.pallas import tpu as pltpu
from jax.sharding import PartitionSpec as P

DEGREES = 5
COMPONENTS = DEGREES * DEGREES
AXES = ("wide", "narrow")


def flat_rows(weights):
    return weights.reshape(weights.shape[0], -1, weights.shape[-1])


def exchange_kernel(
    sizes,
    coefficient_ref,
    features_ref,
    *refs,
):
    wide, narrow, count = sizes
    stacks = refs[:count]
    sides_ref, share_ref = refs[count : count + 2]
    staged = refs[count + 2 : 2 * count + 2]
    partial_ref, received_ref, load_sem, halo_send, halo_recv, send_sem, recv_sem = refs[
        2 * count + 2 :
    ]
    my_wide = lax.axis_index("wide")
    my_narrow = lax.axis_index("narrow")
    part = partial_ref.shape[0] // wide

    loads = []
    for at, (stack, stage) in enumerate(zip(stacks, staged)):
        rows = stage.shape[1]
        loads.append(
            pltpu.make_async_copy(
                stack.at[:, pl.ds(pl.multiple_of(my_narrow * rows, 16), rows), :],
                stage,
                load_sem.at[at],
            )
        )
        loads[-1].start()

    total = wide * narrow
    me = my_wide * narrow + my_narrow
    after = lax.rem(me + 1, total)
    before = lax.rem(me + total - 1, total)
    place = lambda flat: (flat // narrow, lax.rem(flat, narrow))
    peers = [(lax.rem(my_wide + hop, wide), my_narrow) for hop in range(1, wide)]
    barrier = pltpu.get_barrier_semaphore()
    for device in [place(after), place(before)] + peers:
        pl.semaphore_signal(
            barrier, inc=1, device_id=device, device_id_type=pl.DeviceIdType.MESH
        )
    pl.semaphore_wait(barrier, wide + 1)

    copies = []
    for side, device in enumerate([place(after), place(before)]):
        copies.append(
            pltpu.make_async_remote_copy(
                src_ref=features_ref,
                dst_ref=sides_ref.at[side],
                send_sem=halo_send.at[side],
                recv_sem=halo_recv.at[side],
                device_id=device,
                device_id_type=pl.DeviceIdType.MESH,
            )
        )

    for copy in copies:
        copy.start()

    offset = 0
    for load, stage in zip(loads, staged):
        load.wait()
        experts, rows, columns = stage.shape
        for block in range(columns // 128):
            lanes = pl.ds(block * 128, 128)
            value = coefficient_ref[0] * stage[0, :, lanes].astype(jnp.float32)
            for expert in range(1, experts):
                value = value + coefficient_ref[expert] * stage[expert, :, lanes].astype(
                    jnp.float32
                )
            partial_ref[pl.ds(offset, rows), :] = value.astype(jnp.bfloat16)
            offset += rows
    if offset < partial_ref.shape[0]:
        rest = partial_ref.shape[0] - offset
        partial_ref[pl.ds(offset, rest), :] = jnp.zeros((rest, 128), jnp.bfloat16)

    for hop, device in enumerate(peers):
        target = device[0]
        copies.append(
            pltpu.make_async_remote_copy(
                src_ref=partial_ref.at[pl.ds(pl.multiple_of(target * part, 16), part), :],
                dst_ref=received_ref.at[hop],
                send_sem=send_sem.at[hop],
                recv_sem=recv_sem.at[hop],
                device_id=device,
                device_id_type=pl.DeviceIdType.MESH,
            )
        )
    for copy in copies[2:]:
        copy.start()
    for copy in copies[2:]:
        copy.wait()
    summed = partial_ref[pl.ds(pl.multiple_of(my_wide * part, 16), part), :].astype(jnp.float32)
    for hop in range(wide - 1):
        summed = summed + received_ref[hop].astype(jnp.float32)
    share_ref[...] = summed.astype(jnp.bfloat16)
    for copy in copies[:2]:
        copy.wait()


def exchange(features, coefficients, stacks):
    wide = lax.axis_size("wide")
    narrow = lax.axis_size("narrow")
    stacks = [flat_rows(w) for w in stacks]
    staged = [(w.shape[0], w.shape[1] // narrow, w.shape[2]) for w in stacks]
    rows = sum(shape[1] * shape[2] // 128 for shape in staged)
    unit = 16 * wide
    rows = -(-rows // unit) * unit
    anywhere = pl.BlockSpec(memory_space=pl.ANY)
    return pl.pallas_call(
        functools.partial(exchange_kernel, (wide, narrow, len(stacks))),
        in_specs=[pl.BlockSpec(memory_space=pltpu.SMEM)] + [anywhere] * (1 + len(stacks)),
        out_specs=[anywhere, pl.BlockSpec(memory_space=pltpu.VMEM)],
        out_shape=[
            jax.ShapeDtypeStruct((2,) + features.shape, features.dtype),
            jax.ShapeDtypeStruct((rows // wide, 128), jnp.bfloat16),
        ],
        scratch_shapes=[pltpu.VMEM(shape, jnp.bfloat16) for shape in staged]
        + [
            pltpu.VMEM((rows, 128), jnp.bfloat16),
            pltpu.VMEM((wide - 1, rows // wide, 128), jnp.bfloat16),
            pltpu.SemaphoreType.DMA((len(stacks),)),
            pltpu.SemaphoreType.DMA((2,)),
            pltpu.SemaphoreType.DMA((2,)),
            pltpu.SemaphoreType.DMA((wide - 1,)),
            pltpu.SemaphoreType.DMA((wide - 1,)),
        ],
        compiler_params=pltpu.CompilerParams(collective_id=0, has_side_effects=True),
        cost_estimate=pl.CostEstimate(flops=10**9, bytes_accessed=10**7, transcendentals=0),
    )(coefficients, features, *stacks)


def order_starts():
    starts = []
    start = 0
    for order in range(DEGREES):
        starts.append(start)
        start += (DEGREES - order) * (1 if order == 0 else 2)
    return starts


def spread_frames(frames_ref, frame_ref):
    for k in range(frames_ref.shape[0]):
        row = frames_ref[pl.ds(k, 1), :]
        frame_ref[k] = jnp.broadcast_to(row, frame_ref.shape[1:]).astype(jnp.bfloat16)


def rotate_kernel(index_ref, frames_ref, radial_ref, features_ref, turned_ref, source_ref, frame_ref):
    channels, lanes = radial_ref.shape
    extended = features_ref.shape[1]
    spread_frames(frames_ref, frame_ref)

    picked = (
        lax.broadcasted_iota(jnp.int32, (extended, lanes), 0) == index_ref[...]
    ).astype(jnp.bfloat16)
    for component in range(COMPONENTS):
        block = pl.ds(component * channels, channels)
        source_ref[block, :] = jnp.dot(
            features_ref[block, :], picked, preferred_element_type=jnp.float32
        ).astype(jnp.bfloat16)

    starts = order_starts()

    def rotate(i, carried):
        row = pl.multiple_of(i * 8, 8)
        tile = lambda place: pl.ds(pl.multiple_of(place * channels + row, 8), 8)
        radial = radial_ref[pl.ds(row, 8), :]
        offset = 0
        for degree in range(DEGREES):
            size = 2 * degree + 1
            xs = [source_ref[tile(degree * degree + q), :] for q in range(size)]
            for p in range(size):
                value = frame_ref[offset + p * size] * xs[0]
                for q in range(1, size):
                    value = value + frame_ref[offset + p * size + q] * xs[q]
                order = abs(p - degree)
                place = starts[order] + degree - order
                if p < degree:
                    place += DEGREES - order
                turned_ref[tile(place), :] = value * radial
            offset += size * size
        return carried

    lax.fori_loop(0, channels // 8, rotate, 0)


def mix_kernel(
    shapes,
    live_ref,
    frames_ref,
    turned_ref,
    merged_ref,
    scale_ref,
    out_ref,
    gated_ref,
    frame_ref,
    total_ref,
    *weight_refs,
):
    step = pl.program_id(0)
    atoms, _, channels = out_ref.shape
    lanes = live_ref.shape[1]
    members = merged_ref.shape[0]
    lane_tiles = lanes // 128
    starts = order_starts()

    @pl.when(step == 0)
    def _():
        total_ref[...] = jnp.zeros_like(total_ref)
        offset = 0
        for weight_ref, (rows, columns) in zip(weight_refs, shapes):
            part = rows // members
            for block in range(columns // 128):
                whole = jnp.concatenate(
                    [merged_ref[m, pl.ds(offset, part), :] for m in range(members)], axis=0
                )
                weight_ref[pl.ds(block * 128, 128), :] = jnp.transpose(whole)
                offset += part

    spread_frames(frames_ref, frame_ref)

    central = jnp.dot(
        weight_refs[0][...],
        turned_ref[pl.ds(0, DEGREES * channels), :],
        preferred_element_type=jnp.float32,
    )
    scalar = central[:channels]
    gate = live_ref[...] / (1.0 + jnp.exp(-scalar))
    for degree in range(DEGREES):
        gated_ref[pl.ds((degree * degree + degree) * channels, channels), :] = (
            central[degree * channels : (degree + 1) * channels] * gate
        ).astype(jnp.bfloat16)
    for order in range(1, DEGREES):
        kept = DEGREES - order
        height = kept * channels
        plus = turned_ref[pl.ds(starts[order] * channels, height), :]
        minus = turned_ref[pl.ds(starts[order] * channels + height, height), :]
        for side in range(2):
            pair = [plus, -minus] if side == 0 else [minus, plus]
            mixed = jnp.dot(
                weight_refs[order][...],
                jnp.concatenate(pair, axis=0),
                preferred_element_type=jnp.float32,
            )
            for column in range(kept):
                degree = order + column
                component = degree * degree + degree + (order if side == 0 else -order)
                gated_ref[pl.ds(component * channels, channels), :] = (
                    mixed[column * channels : (column + 1) * channels] * gate
                ).astype(jnp.bfloat16)

    def unrotate(i, carried):
        row = pl.multiple_of(i * 8, 8)
        tile = lambda place: pl.ds(pl.multiple_of(place * channels + row, 8), 8)
        offset = 0
        for degree in range(DEGREES):
            size = 2 * degree + 1
            ys = [gated_ref[tile(degree * degree + q), :] for q in range(size)]
            for p in range(size):
                value = frame_ref[offset + p] * ys[0]
                for q in range(1, size):
                    value = value + frame_ref[offset + q * size + p] * ys[q]
                value = value.astype(jnp.float32)
                place = tile(degree * degree + p)
                summed = total_ref[place, :]
                for part in range(lane_tiles):
                    summed = summed + value[:, part * 128 : (part + 1) * 128]
                total_ref[place, :] = summed
            offset += size * size
        return carried

    lax.fori_loop(0, channels // 8, unrotate, 0)

    @pl.when(step == pl.num_programs(0) - 1)
    def _():
        for component in range(COMPONENTS):
            block = jnp.transpose(total_ref[pl.ds(component * channels, channels), :])
            total = block[:atoms]
            for part in range(1, 128 // atoms):
                total = total + block[part * atoms : (part + 1) * atoms]
            out_ref[:, component, :] = total * scale_ref[...]


def body(
    node_features,
    frames,
    radial,
    neighbours,
    counts,
    coefficients,
    w_zero,
    w_one,
    w_two,
    w_three,
    w_four,
):
    atoms, components, channels = node_features.shape
    slots = neighbours.shape[1]
    entries = frames.shape[2]
    edges = atoms * slots
    stacks = (w_zero, w_one, w_two, w_three, w_four)
    sides, share = exchange(node_features, coefficients, stacks)
    merged = lax.all_gather(
        lax.all_gather(share, "narrow", axis=0, tiled=False), "wide", axis=1, tiled=False
    )
    merged = merged.reshape(lax.axis_size("narrow"), -1, 128)
    shapes = [(int(np.prod(w.shape[1:-1])), w.shape[-1]) for w in stacks]

    features = jnp.concatenate([sides[0], node_features, sides[1]], axis=0)
    features = features.reshape(3 * atoms, components * channels).T
    block_start = lax.axis_index(AXES) * atoms
    atoms_total = atoms * lax.axis_size(AXES)
    index = ((neighbours - block_start + atoms) % atoms_total).T.reshape(1, edges)
    live = (lax.broadcasted_iota(jnp.int32, (slots, atoms), 0) < counts[None, :]).astype(
        jnp.float32
    ).reshape(1, edges)
    frames_t = frames.transpose(2, 1, 0).reshape(entries, edges).astype(jnp.float32)
    radial_t = radial.transpose(2, 1, 0).reshape(channels, edges)
    scale = jnp.broadcast_to(
        (1.0 / jnp.sqrt(counts.astype(jnp.float32)))[:, None], (atoms, channels)
    )

    lanes = 256
    whole = lambda shape: pl.BlockSpec(shape, lambda i: (0,) * len(shape))
    columns = lambda rows: pl.BlockSpec((rows, lanes), lambda i: (0, i))
    params = pltpu.CompilerParams(
        dimension_semantics=("arbitrary",), vmem_limit_bytes=56 * 1024 * 1024
    )
    turned = pl.pallas_call(
        rotate_kernel,
        grid=(edges // lanes,),
        in_specs=[columns(1), columns(entries), columns(channels), whole(features.shape)],
        out_specs=columns(components * channels),
        out_shape=jax.ShapeDtypeStruct((components * channels, edges), jnp.bfloat16),
        scratch_shapes=[
            pltpu.VMEM((components * channels, lanes), jnp.bfloat16),
            pltpu.VMEM((entries, 8, lanes), jnp.bfloat16),
        ],
        compiler_params=params,
        cost_estimate=pl.CostEstimate(
            flops=2 * 3 * atoms * components * channels * edges,
            bytes_accessed=2 * components * channels * edges,
            transcendentals=0,
        ),
    )(index, frames_t, radial_t, features)
    return pl.pallas_call(
        functools.partial(mix_kernel, shapes),
        grid=(edges // lanes,),
        in_specs=[
            columns(1),
            columns(entries),
            columns(components * channels),
            whole(merged.shape),
            whole(scale.shape),
        ],
        out_specs=whole((atoms, components, channels)),
        out_shape=jax.ShapeDtypeStruct((atoms, components, channels), jnp.float32),
        scratch_shapes=[
            pltpu.VMEM((components * channels, lanes), jnp.bfloat16),
            pltpu.VMEM((entries, 8, lanes), jnp.bfloat16),
            pltpu.VMEM((components * channels, 128), jnp.float32),
        ]
        + [pltpu.VMEM((n, k), jnp.bfloat16) for k, n in shapes],
        compiler_params=params,
    )(live, frames_t, turned, merged, scale)


def solution(mesh):
    spread = lambda rest: P(AXES, *([None] * rest))
    in_specs = (
        spread(2),
        spread(2),
        spread(2),
        spread(1),
        spread(0),
        P("wide"),
        P("wide", None, None),
        P("wide", None, None, None),
        P("wide", None, None, None),
        P("wide", None, None, None),
        P("wide", None, None, None),
    )
    return jax.shard_map(body, mesh=mesh, in_specs=in_specs, out_specs=spread(2), check_vma=False)
```

profile of v0, /device:TPU:0, one launch (start us, length us, event | category | flops | bytes accessed | tf_op | source)
XLA Modules:
  0.0 143.2 jit_solution(10306671922315509816)
XLA Ops:
  6.5 0.0 all-gather.4.cloned.1.call-start
  6.5 2.1 %copy.21.features_ref = bf16[64,25,128]{2,1,0:T(8,128)(2,1)} copy(bf16[64,25,128]{2,0,1:T(8,128)(2,1)} %param.11) | data formatting | bytes 819200 | tf_op args[0]
  8.6 0.0 copy-start.3
  8.6 31.0 %shard_map.109 = (bf16[2,64,25,128]{3,2,1,0:T(8,128)(2,1)}, bf16[352,128]{1,0:T(8,128)(2,1)}) custom-call(f32[4]{0:T(128)} %coefficient_ref.1, bf16[64,25,128]{2,1,0:T(8,128)(2,1)} %copy.21.features_ref, bf16[4,640,640]{2,1,0:T(8,128)(2,1)} %refs_0_.1, bf16[4,1024,512]{2,1,0:T(8,128)(2,1)} %bitcast.19, bf16[4,768,384]{2,1,0:T(8,128)(2,1)} %bitcast.24, ...), custom_call_target="tpu_custom_call" | custom-call | flops 1000000000 | bytes 10000000 | tf_op jit(solution)/shard_map/pallas_call | solution.py:128
  39.6 16.3 %all-gather = bf16[1408,128]{1,0:T(8,128)(2,1)} all-gather(bf16[352,128]{1,0:T(8,128)(2,1)} %get-tuple-element.8), channel_id=2, replica_groups=mesh['wide'=8,'narrow'=4] {'narrow'}, dimensions={0}, use_global_device_ids=true | all-gather | bytes 450560 | tf_op jit(solution)/shard_map/all_gather | solution.py:322
  55.9 0.0 copy-start.5
  55.9 0.0 all-gather.4.cloned.1.call-update
  55.9 0.0 copy-done.3
  55.9 0.0 copy-start.4
  55.9 1.3 copy.23
  57.2 1.3 fusion.3
  58.5 1.5 %copy.24 = bf16[1,64,25,128]{1,3,2,0:T(8,128)(2,1)} copy(bf16[1,64,25,128]{3,2,1,0:T(8,128)(2,1)S(1)} %get-tuple-element.10) | data formatting | bytes 819200 | tf_op jit(solution)/shard_map/slice | solution.py:327
  59.9 1.5 %copy.22 = bf16[1,64,25,128]{1,3,2,0:T(8,128)(2,1)} copy(bf16[1,64,25,128]{3,2,1,0:T(8,128)(2,1)S(1)} %get-tuple-element.9) | data formatting | bytes 819200 | tf_op jit(solution)/shard_map/slice | solution.py:327
  61.4 0.0 copy-done.5
  61.4 0.7 reshape.60.index_ref
  62.1 0.0 copy-done.4
  62.1 0.4 convert_bitcast_fusion
  62.5 1.8 %copy.19 = f32[165,48,64]{0,2,1:T(8,128)S(1)} copy(f32[165,48,64]{0,1,2:T(8,128)S(1)} %convert_bitcast_fusion) | data formatting | bytes 4055040 | tf_op jit(solution)/shard_map/convert_element_type | solution.py:335
  64.4 0.0 copy-start.6
  64.4 2.1 %copy.27.frames_ref = f32[165,3072]{1,0:T(8,128)} copy(f32[165,3072]{0,1:T(8,128)S(1)} %bitcast.18) | data formatting | bytes 4055040 | tf_op jit(solution)/shard_map/convert_element_type | solution.py:335
  66.5 0.0 copy-start
  66.5 0.0 copy-start.1
  66.5 0.0 copy-start.2
  66.5 1.5 %copy.20 = bf16[64,48,128]{2,0,1:T(8,128)(2,1)S(1)} copy(bf16[64,48,128]{2,1,0:T(8,128)(2,1)} %param.13) | data formatting | bytes 1572864 | tf_op args[2]
  68.0 1.2 copy.26.radial_ref
  69.1 0.0 copy-done.6
  69.1 0.7 reshape.67.live_ref
  69.8 0.0 copy-done
  69.8 0.0 copy-done.1
  69.8 0.0 copy-done.2
  69.9 2.1 %maximum_bitcast_fusion.features_ref = bf16[3200,192]{1,0:T(8,128)(2,1)} fusion(bf16[64,3200]{0,1:T(8,128)(2,1)S(1)} %bitcast.21, bf16[64,3200]{0,1:T(8,128)(2,1)S(1)} %bitcast.20, bf16[64,3200]{0,1:T(8,128)(2,1)S(1)} %bitcast.22), kind=kLoop, calls=%fused_computation.1 | loop fusion | flops 3686400 | bytes 2457600 | tf_op jit(solution)/shard_map/transpose | solution.py:328
  71.9 22.7 %shard_map.110.turned_ref = bf16[3200,3072]{1,0:T(8,128)(2,1)} custom-call(s32[1,3072]{1,0:T(1,128)} %reshape.60.index_ref, f32[165,3072]{1,0:T(8,128)} %copy.27.frames_ref, bf16[128,3072]{1,0:T(8,128)(2,1)} %copy.26.radial_ref, bf16[3200,192]{1,0:T(8,128)(2,1)} %maximum_bitcast_fusion.features_ref), custom_call_target="tpu_custom_call" | custom-call | flops 3774873600 | bytes 19660800 | tf_op jit(solution)/shard_map/pallas_call | solution.py:347
  94.7 0.0 all-gather.4.cloned.1.call-done.merged_ref
  94.7 0.7 broadcast_in_dim.2.scale_ref
  95.3 38.4 %shard_map.111 = f32[64,25,128]{2,1,0:T(8,128)} custom-call(f32[1,3072]{1,0:T(1,128)} %reshape.67.live_ref, f32[165,3072]{1,0:T(8,128)} %copy.27.frames_ref, bf16[3200,3072]{1,0:T(8,128)(2,1)} %shard_map.110.turned_ref, bf16[4,2816,128]{2,1,0:T(8,128)(2,1)} %all-gather.4.cloned.1.call-done.merged_ref, f32[64,128]{1,0:T(8,128)} %broadcast_in_dim.2.scale_ref), custom_call_target="tpu_custom_call" | custom-call | tf_op jit(solution)/shard_map/pallas_call | solution.py:364
  133.7 2.6 %copy.28 = f32[64,25,128]{2,0,1:T(8,128)} copy(f32[64,25,128]{2,1,0:T(8,128)} %shard_map.111) | data formatting | bytes 1638400 | tf_op jit(solution)/shard_map/pallas_call | solution.py:364
  (3 shorter events, 0.0 us)
Async XLA Ops:
  6.5 88.1 %all-gather.4.cloned.1.call-start = ((), (), s32[]{:S(2)}) async-start(), calls=%async_computation | async-start | bytes 3244032 | tf_op jit(solution)/shard_map/all_gather | solution.py:321
  8.6 47.3 %copy-start.3 = (bf16[64,25,128]{2,0,1:T(8,128)(2,1)S(1)}, bf16[64,25,128]{2,0,1:T(8,128)(2,1)}, u32[]{:S(2)}) copy-start(bf16[64,25,128]{2,0,1:T(8,128)(2,1)} %param.11) | copy-start | bytes 1228804
  55.9 5.5 %copy-start.5 = (s32[64,48]{0,1:T(8,128)S(1)}, s32[64,48]{0,1:T(8,128)}, u32[]{:S(2)}) copy-start(s32[64,48]{0,1:T(8,128)} %param.14) | copy-start | bytes 36868
  55.9 6.2 %copy-start.4 = (bf16[64,48,165]{2,1,0:T(8,128)(2,1)S(1)}, bf16[64,48,165]{2,1,0:T(8,128)(2,1)}, u32[]{:S(2)}) copy-start(bf16[64,48,165]{2,1,0:T(8,128)(2,1)} %param.12) | copy-start | bytes 3041284
  64.4 4.8 %copy-start.6 = (s32[64]{0:T(128)S(1)}, s32[64]{0:T(128)}, u32[]{:S(2)}) copy-start(s32[64]{0:T(128)} %param.15) | copy-start | bytes 772
  66.5 3.4 %copy-start = (bf16[64,25,128]{0,2,1:T(8,128)(2,1)S(1)}, bf16[64,25,128]{0,2,1:T(8,128)(2,1)}, u32[]{:S(2)}) copy-start(bf16[64,25,128]{0,2,1:T(8,128)(2,1)} %copy.23) | copy-start | bytes 1228804
  66.5 3.4 %copy-start.1 = (bf16[1,64,25,128]{1,3,2,0:T(8,128)(2,1)S(1)}, bf16[1,64,25,128]{1,3,2,0:T(8,128)(2,1)}, u32[]{:S(2)}) copy-start(bf16[1,64,25,128]{1,3,2,0:T(8,128)(2,1)} %copy.24) | copy-start | bytes 1228804
  66.5 3.4 %copy-start.2 = (bf16[1,64,25,128]{1,3,2,0:T(8,128)(2,1)S(1)}, bf16[1,64,25,128]{1,3,2,0:T(8,128)(2,1)}, u32[]{:S(2)}) copy-start(bf16[1,64,25,128]{1,3,2,0:T(8,128)(2,1)} %copy.22) | copy-start | bytes 1228804
Sparse Core Ops, SparseCore 0:
  56.0 31.0 all-gather.3
where the time goes:
time: 143 us
  Pallas kernels  92.1 us (64%)
  local copies, waits for them, and re-layouts  18.8 us (13%)
  blocking collectives  16.3 us (11%)
  between operations  13.5 us (9%)
  other arithmetic  2.51 us (2%)
    pallas_call x1, Pallas kernels, body(): pl.pallas_call(functools.partial(mix_kernel, shapes), grid=(edges // lane...  38.4 us
    pallas_call x1, Pallas kernels, exchange(): pl.pallas_call(functools.partial(exchange_kernel, (wide, narrow, len(stac...  31 us
    pallas_call x1, Pallas kernels, body(): pl.pallas_call(rotate_kernel, grid=(edges // lanes,), in_specs=[columns(1...  22.7 us
    all_gather x1, blocking collectives, body(): lax.all_gather(share, 'narrow', axis=0, tiled=False)  16.3 us
    unnamed x17, local copies, waits for them, and re-layouts  4.85 us
    slice x3, local copies, waits for them, and re-layouts, body(): features = jnp.concatenate([sides[0], node_features, sides[1]], axis=0)  4.19 us
    convert_element_type x2, local copies, waits for them, and re-layouts, body(): frames.transpose(2, 1, 0).reshape(entries, edges).astype(jnp.float32)  3.93 us
  transfers between devices with their start and end apart: 1, of which 0 were waited for; matrix products, arithmetic and copies ran while one was open for 11% of the time, Pallas kernels for 16%

commit v1 on v0

v1 whole, which is shorter than its diff:
```python
import functools

import jax
import jax.numpy as jnp
import numpy as np
from jax import lax
from jax.experimental import pallas as pl
from jax.experimental.pallas import tpu as pltpu
from jax.sharding import PartitionSpec as P

DEGREES = 5
COMPONENTS = DEGREES * DEGREES
AXES = ("wide", "narrow")
MESH = pl.DeviceIdType.MESH


def flat_rows(weights):
    return weights.reshape(weights.shape[0], -1, weights.shape[-1])


def remote(src, dst, send, recv, device):
    return pltpu.make_async_remote_copy(
        src_ref=src,
        dst_ref=dst,
        send_sem=send,
        recv_sem=recv,
        device_id=device,
        device_id_type=MESH,
    )


def exchange_kernel(sizes, coefficient_ref, features_ref, *refs):
    wide, narrow, count = sizes
    stacks = refs[:count]
    sides_ref, merged_ref = refs[count : count + 2]
    staged = refs[count + 2 : 2 * count + 2]
    (
        partial_ref,
        received_ref,
        share_ref,
        load_sem,
        halo_send,
        halo_recv,
        send_sem,
        recv_sem,
        line_send,
        line_recv,
        plane_send,
        plane_recv,
        pair_send,
        pair_recv,
        local_sem,
    ) = refs[2 * count + 2 :]
    my_wide = lax.axis_index("wide")
    my_narrow = lax.axis_index("narrow")
    part = partial_ref.shape[0] // wide
    chips = wide // 2
    my_chip = my_wide // 2
    my_core = lax.rem(my_wide, 2)

    loads = []
    for at, (stack, stage) in enumerate(zip(stacks, staged)):
        rows = stage.shape[1]
        loads.append(
            pltpu.make_async_copy(
                stack.at[:, pl.ds(pl.multiple_of(my_narrow * rows, 16), rows), :],
                stage,
                load_sem.at[at],
            )
        )
        loads[-1].start()

    total = wide * narrow
    me = my_wide * narrow + my_narrow
    after = lax.rem(me + 1, total)
    before = lax.rem(me + total - 1, total)
    place = lambda flat: (flat // narrow, lax.rem(flat, narrow))
    peers = [(lax.rem(my_wide + hop, wide), my_narrow) for hop in range(1, wide)]
    line = [(my_wide, lax.rem(my_narrow + hop, narrow)) for hop in range(1, narrow)]
    greeted = [place(after), place(before)] + peers + line
    barrier = pltpu.get_barrier_semaphore()
    for device in greeted:
        pl.semaphore_signal(barrier, inc=1, device_id=device, device_id_type=MESH)
    pl.semaphore_wait(barrier, len(greeted))

    halo = []
    for side, device in enumerate([place(after), place(before)]):
        halo.append(
            remote(
                features_ref, sides_ref.at[side], halo_send.at[side], halo_recv.at[side], device
            )
        )
        halo[-1].start()

    offset = 0
    for load, stage in zip(loads, staged):
        load.wait()
        experts, rows, columns = stage.shape
        for block in range(columns // 128):
            lanes = pl.ds(block * 128, 128)
            value = coefficient_ref[0] * stage[0, :, lanes].astype(jnp.float32)
            for expert in range(1, experts):
                value = value + coefficient_ref[expert] * stage[expert, :, lanes].astype(
                    jnp.float32
                )
            partial_ref[pl.ds(offset, rows), :] = value.astype(jnp.bfloat16)
            offset += rows
    if offset < partial_ref.shape[0]:
        rest = partial_ref.shape[0] - offset
        partial_ref[pl.ds(offset, rest), :] = jnp.zeros((rest, 128), jnp.bfloat16)

    scatter = []
    for hop, device in enumerate(peers):
        target = device[0]
        scatter.append(
            remote(
                partial_ref.at[pl.ds(pl.multiple_of(target * part, 16), part), :],
                received_ref.at[hop],
                send_sem.at[hop],
                recv_sem.at[hop],
                device,
            )
        )
        scatter[-1].start()
    summed = partial_ref[pl.ds(pl.multiple_of(my_wide * part, 16), part), :].astype(jnp.float32)
    for hop in range(wide - 1):
        scatter[hop].wait_recv()
        summed = summed + received_ref[hop].astype(jnp.float32)
    share_ref[...] = summed.astype(jnp.bfloat16)

    keep = pltpu.make_async_copy(share_ref, merged_ref.at[my_narrow, my_wide], local_sem)
    keep.start()
    partner = (my_wide + 1 - 2 * my_core, my_narrow)
    along = []
    for hop in range(1, narrow):
        along.append(
            remote(
                share_ref,
                merged_ref.at[my_narrow, my_wide],
                line_send.at[hop - 1],
                line_recv.at[hop - 1],
                line[hop - 1],
            )
        )
        along[-1].start()
    across = []
    paired = []

    def forward(hop):
        origin = lax.rem(my_narrow + narrow - hop, narrow)
        slot = merged_ref.at[origin, my_wide]
        source = share_ref if hop == 0 else slot
        for step in range(1, chips):
            at = hop * (chips - 1) + step - 1
            target = lax.rem(my_chip + step, chips) * 2 + my_core
            across.append(
                remote(source, slot, plane_send.at[at], plane_recv.at[at], (target, my_narrow))
            )
            across[-1].start()
        at = hop * chips
        paired.append(remote(source, slot, pair_send.at[at], pair_recv.at[at], partner))
        paired[-1].start()

    def relay(hop):
        origin = lax.rem(my_narrow + narrow - hop, narrow)
        for step in range(1, chips):
            across[hop * (chips - 1) + step - 1].wait_recv()
            owner = lax.rem(my_chip + chips - step, chips) * 2 + my_core
            slot = merged_ref.at[origin, owner]
            at = hop * chips + step
            paired.append(remote(slot, slot, pair_send.at[at], pair_recv.at[at], partner))
            paired[-1].start()

    forward(0)
    for hop in range(1, narrow):
        along[hop - 1].wait_recv()
        forward(hop)
    for hop in range(narrow):
        relay(hop)
    for copy in paired:
        copy.wait_recv()
    for copy in scatter + along + across + paired:
        copy.wait_send()
    keep.wait()
    for copy in halo:
        copy.wait()


def exchange(features, coefficients, stacks):
    wide = lax.axis_size("wide")
    narrow = lax.axis_size("narrow")
    stacks = [flat_rows(w) for w in stacks]
    staged = [(w.shape[0], w.shape[1] // narrow, w.shape[2]) for w in stacks]
    rows = sum(shape[1] * shape[2] // 128 for shape in staged)
    unit = 16 * wide
    rows = -(-rows // unit) * unit
    part = rows // wide
    chips = wide // 2
    anywhere = pl.BlockSpec(memory_space=pl.ANY)
    dma = lambda n: pltpu.SemaphoreType.DMA((n,))
    return pl.pallas_call(
        functools.partial(exchange_kernel, (wide, narrow, len(stacks))),
        in_specs=[pl.BlockSpec(memory_space=pltpu.SMEM)] + [anywhere] * (1 + len(stacks)),
        out_specs=[anywhere, anywhere],
        out_shape=[
            jax.ShapeDtypeStruct((2,) + features.shape, features.dtype),
            jax.ShapeDtypeStruct((narrow, wide, part, 128), jnp.bfloat16),
        ],
        scratch_shapes=[pltpu.VMEM(shape, jnp.bfloat16) for shape in staged]
        + [
            pltpu.VMEM((rows, 128), jnp.bfloat16),
            pltpu.VMEM((wide - 1, part, 128), jnp.bfloat16),
            pltpu.VMEM((part, 128), jnp.bfloat16),
            dma(len(stacks)),
            dma(2),
            dma(2),
            dma(wide - 1),
            dma(wide - 1),
            dma(narrow - 1),
            dma(narrow - 1),
            dma(narrow * (chips - 1)),
            dma(narrow * (chips - 1)),
            dma(narrow * chips),
            dma(narrow * chips),
            pltpu.SemaphoreType.DMA,
        ],
        compiler_params=pltpu.CompilerParams(collective_id=0, has_side_effects=True),
    )(coefficients, features, *stacks)


def order_starts():
    starts = []
    start = 0
    for order in range(DEGREES):
        starts.append(start)
        start += (DEGREES - order) * (1 if order == 0 else 2)
    return starts


def turn(xs, frame_ref, radial, turned_ref, tile):
    starts = order_starts()
    offset = 0
    for degree in range(DEGREES):
        size = 2 * degree + 1
        base = degree * degree
        for p in range(size):
            value = frame_ref[offset + p * size] * xs(base)
            for q in range(1, size):
                value = value + frame_ref[offset + p * size + q] * xs(base + q)
            order = abs(p - degree)
            at = starts[order] + degree - order
            if p < degree:
                at += DEGREES - order
            turned_ref[tile(at), :] = value * radial
        offset += size * size


def convolve_kernel(
    shapes,
    slots,
    neighbours_ref,
    counts_ref,
    frames_ref,
    radial_ref,
    features_ref,
    sides_ref,
    merged_ref,
    out_ref,
    extended_ref,
    rows_ref,
    source_ref,
    frame_ref,
    spread_ref,
    radial_t_ref,
    turned_ref,
    gated_ref,
    total_ref,
    column_ref,
    *weight_refs,
):
    step = pl.program_id(0)
    components, atoms, channels = out_ref.shape
    lanes, entries = frames_ref.shape
    members = merged_ref.shape[0]
    starts = order_starts()
    iota = lambda shape, axis: lax.broadcasted_iota(jnp.int32, shape, axis)

    @pl.when(step == 0)
    def _():
        total_ref[...] = jnp.zeros_like(total_ref)
        for component in range(components):
            stacked = jnp.concatenate(
                [sides_ref[0, component], features_ref[component], sides_ref[1, component]], axis=0
            )
            extended_ref[pl.ds(component * channels, channels), :] = jnp.transpose(stacked)
        wide, narrow = lax.axis_size("wide"), lax.axis_size("narrow")
        start = (lax.axis_index("wide") * narrow + lax.axis_index("narrow")) * atoms
        everything = atoms * wide * narrow
        relative = neighbours_ref[...] - (start - atoms)
        relative = jnp.where(relative < 0, relative + everything, relative)
        relative = jnp.where(relative >= everything, relative - everything, relative)
        relative = jnp.minimum(relative, 255)
        rows_ref[...] = relative.astype(jnp.float32).astype(jnp.bfloat16)
        square = (atoms, atoms)
        diagonal = iota(square, 0) == iota(square, 1)
        count = jnp.sum(
            jnp.where(diagonal, counts_ref[...].astype(jnp.float32), 0.0), axis=1, keepdims=True
        )
        column_ref[...] = jnp.broadcast_to(count, column_ref.shape)
        offset = 0
        for weight_ref, (rows, columns) in zip(weight_refs, shapes):
            part = rows // members
            for block in range(columns // 128):
                whole = jnp.concatenate(
                    [merged_ref[m, pl.ds(offset, part), :] for m in range(members)], axis=0
                )
                weight_ref[pl.ds(block * 128, 128), :] = jnp.transpose(whole)
                offset += part

    edge = iota((1, lanes), 1) + step * lanes
    home = edge // slots
    slot = edge - home * slots

    chosen = (iota((atoms, lanes), 0) == home).astype(jnp.bfloat16)
    spread = jnp.dot(rows_ref[...], chosen, preferred_element_type=jnp.float32)
    index = jnp.sum(
        jnp.where(iota((slots, lanes), 0) == slot, spread, 0.0), axis=0, keepdims=True
    ).astype(jnp.int32)
    extended = extended_ref.shape[1]
    picked = (iota((extended, lanes), 0) == index).astype(jnp.bfloat16)
    for component in range(components):
        block = pl.ds(component * channels, channels)
        source_ref[block, :] = jnp.dot(
            extended_ref[block, :], picked, preferred_element_type=jnp.float32
        ).astype(jnp.bfloat16)

    padded = frame_ref.shape[0]
    eye = (iota((padded, entries), 0) == iota((padded, entries), 1)).astype(jnp.bfloat16)
    across = (((1,), (1,)), ((), ()))
    frame_ref[...] = lax.dot_general(
        eye, frames_ref[...], across, preferred_element_type=jnp.float32
    )
    eye = (iota((channels, channels), 0) == iota((channels, channels), 1)).astype(jnp.bfloat16)
    radial_t_ref[...] = lax.dot_general(
        eye, radial_ref[...], across, preferred_element_type=jnp.float32
    ).astype(jnp.bfloat16)
    for k in range(entries):
        row = frame_ref[pl.ds(k, 1), :]
        spread_ref[k] = jnp.broadcast_to(row, spread_ref.shape[1:]).astype(jnp.bfloat16)

    height = spread_ref.shape[1]

    def rotate(i, carried):
        row = pl.multiple_of(i * height, height)
        tile = lambda place: pl.ds(pl.multiple_of(place * channels + row, height), height)
        turn(
            lambda q: source_ref[tile(q), :],
            spread_ref,
            radial_t_ref[pl.ds(row, height), :],
            turned_ref,
            tile,
        )
        return carried

    lax.fori_loop(0, channels // height, rotate, 0)

    central = jnp.dot(
        weight_refs[0][...],
        turned_ref[pl.ds(0, DEGREES * channels), :],
        preferred_element_type=jnp.float32,
    )
    gate = 1.0 / (1.0 + jnp.exp(-central[:channels]))
    for degree in range(DEGREES):
        gated_ref[pl.ds((degree * degree + degree) * channels, channels), :] = (
            central[degree * channels : (degree + 1) * channels] * gate
        ).astype(jnp.bfloat16)
    for order in range(1, DEGREES):
        kept = DEGREES - order
        tall = kept * channels
        plus = turned_ref[pl.ds(starts[order] * channels, tall), :]
        minus = turned_ref[pl.ds(starts[order] * channels + tall, tall), :]
        for side in range(2):
            pair = [plus, -minus] if side == 0 else [minus, plus]
            mixed = jnp.dot(
                weight_refs[order][...],
                jnp.concatenate(pair, axis=0),
                preferred_element_type=jnp.float32,
            )
            for column in range(kept):
                degree = order + column
                component = degree * degree + degree + (order if side == 0 else -order)
                gated_ref[pl.ds(component * channels, channels), :] = (
                    mixed[column * channels : (column + 1) * channels] * gate
                ).astype(jnp.bfloat16)

    window = 8
    first = jnp.minimum((step * lanes) // slots, atoms - window)
    position = slot + slots * (home - first) - slots * iota((window, lanes), 0)
    count = column_ref[pl.ds(first, window), :]
    count = jnp.concatenate([count] * (lanes // channels), axis=1)
    live = jnp.where(
        (position >= 0) & (position.astype(jnp.float32) < count) & (position < slots), 1.0, 0.0
    )
    offset = 0
    for degree in range(DEGREES):
        size = 2 * degree + 1
        summed = None
        for q in range(size):
            left = jnp.concatenate(
                [
                    jnp.broadcast_to(frame_ref[pl.ds(offset + q * size + p, 1), :], live.shape) * live
                    for p in range(size)
                ],
                axis=0,
            ).astype(jnp.bfloat16)
            block = pl.ds((degree * degree + q) * channels, channels)
            term = lax.dot_general(
                left, gated_ref[block, :], across, preferred_element_type=jnp.float32
            )
            summed = term if summed is None else summed + term
        for p in range(size):
            at = degree * degree + p
            total_ref[at, pl.ds(first, window), :] = (
                total_ref[at, pl.ds(first, window), :] + summed[p * window : (p + 1) * window]
            )
        offset += size * size

    @pl.when(step == pl.num_programs(0) - 1)
    def _():
        scale = 1.0 / jnp.sqrt(column_ref[...])
        for component in range(components):
            out_ref[component] = total_ref[component] * scale


def body(
    node_features,
    frames,
    radial,
    neighbours,
    counts,
    coefficients,
    w_zero,
    w_one,
    w_two,
    w_three,
    w_four,
):
    atoms, components, channels = node_features.shape
    slots = neighbours.shape[1]
    entries = frames.shape[2]
    edges = atoms * slots
    stacks = (w_zero, w_one, w_two, w_three, w_four)
    features = node_features.transpose(1, 0, 2)
    sides, merged = exchange(features, coefficients, stacks)
    merged = merged.reshape(merged.shape[0], -1, 128)
    shapes = [(int(np.prod(w.shape[1:-1])), w.shape[-1]) for w in stacks]

    lanes = 256
    height = 16
    padded = -(-entries // 16) * 16
    whole = lambda shape: pl.BlockSpec(shape, lambda i: (0,) * len(shape))
    rows = lambda width: pl.BlockSpec((lanes, width), lambda i: (i, 0))
    out = pl.pallas_call(
        functools.partial(convolve_kernel, shapes, slots),
        grid=(edges // lanes,),
        in_specs=[
            whole((slots, atoms)),
            whole((1, atoms)),
            rows(entries),
            rows(channels),
            whole(features.shape),
            whole(sides.shape),
            whole(merged.shape),
        ],
        out_specs=whole((components, atoms, channels)),
        out_shape=jax.ShapeDtypeStruct((components, atoms, channels), jnp.float32),
        scratch_shapes=[
            pltpu.VMEM((components * channels, 3 * atoms), jnp.bfloat16),
            pltpu.VMEM((slots, atoms), jnp.bfloat16),
            pltpu.VMEM((components * channels, lanes), jnp.bfloat16),
            pltpu.VMEM((padded, lanes), jnp.float32),
            pltpu.VMEM((entries, height, lanes), jnp.bfloat16),
            pltpu.VMEM((channels, lanes), jnp.bfloat16),
            pltpu.VMEM((components * channels, lanes), jnp.bfloat16),
            pltpu.VMEM((components * channels, lanes), jnp.bfloat16),
            pltpu.VMEM((components, atoms, channels), jnp.float32),
            pltpu.VMEM((atoms, channels), jnp.float32),
        ]
        + [pltpu.VMEM((n, k), jnp.bfloat16) for k, n in shapes],
        compiler_params=pltpu.CompilerParams(
            dimension_semantics=("arbitrary",), vmem_limit_bytes=56 * 1024 * 1024
        ),
    )(
        neighbours.T,
        counts.reshape(1, atoms),
        frames.reshape(edges, entries),
        radial.reshape(edges, channels),
        features,
        sides,
        merged,
    )
    return out.transpose(1, 0, 2)


def solution(mesh):
    spread = lambda rest: P(AXES, *([None] * rest))
    in_specs = (
        spread(2),
        spread(2),
        spread(2),
        spread(1),
        spread(0),
        P("wide"),
        P("wide", None, None),
        P("wide", None, None, None),
        P("wide", None, None, None),
        P("wide", None, None, None),
        P("wide", None, None, None),
    )
    return jax.shard_map(body, mesh=mesh, in_specs=in_specs, out_specs=spread(2), check_vma=False)
```

time: 143 us -> 93.6 us (0.65)
  local copies, waits for them, and re-layouts: 18.8 us -> 0 us
  blocking collectives: 16.3 us -> 0 us
  between operations: 13.5 us -> 0.01 us
  other arithmetic: 2.51 us -> 0 us
    all_gather x1 -> x0, blocking collectives: 16.3 us -> none  [body(): lax.all_gather(share, 'narrow', axis=0, tiled=False)]
    pallas_call x1, Pallas kernels: 31 us -> 44.1 us  [exchange(): pl.pallas_call(functools.partial(exchange_kernel, (wide, narrow, len(stac...]
    pallas_call x2 -> x1, Pallas kernels: 61.1 us -> 49.4 us  [body(): pl.pallas_call(functools.partial(convolve_kernel, shapes, slots), grid=(e...]
    unnamed x17 -> x0, local copies, waits for them, and re-layouts: 4.85 us -> none
    convert_element_type x3 -> x0, local copies, waits for them, and re-layouts: 4.61 us -> none  [the longest x2 3.93 us: body(): frames.transpose(2, 1, 0).reshape(entries, edges).astype(jnp.float32)]
    slice x3 -> x0, local copies, waits for them, and re-layouts: 4.19 us -> none  [body(): features = jnp.concatenate([sides[0], node_features, sides[1]], axis=0)]
    pallas_call x1 -> x0, local copies, waits for them, and re-layouts: 2.59 us -> none  [body(): pl.pallas_call(functools.partial(mix_kernel, shapes), grid=(edges // lane...]
    transpose x2 -> x0, other arithmetic: 2.08 us -> none  [the longest x1 2.07 us: body(): features = features.reshape(3 * atoms, components * channels).T]
  transfers between devices with their start and end apart: 1 -> 0, of which waited for: 0 -> 0; matrix products, arithmetic and copies ran while one was open for 11% -> 0% of each run, Pallas kernels for 16% -> 0%
where the time goes in v1:
time: 93.6 us; the launch traced here: 93.5 us
  Pallas kernels  93.5 us (100%)
    pallas_call x1, Pallas kernels, body(): pl.pallas_call(functools.partial(convolve_kernel, shapes, slots), grid=(e...  49.4 us
    pallas_call x1, Pallas kernels, exchange(): pl.pallas_call(functools.partial(exchange_kernel, (wide, narrow, len(stac...  44.1 us

profile of v1, /device:TPU:0, one launch (start us, length us, event | category | flops | bytes accessed | tf_op | source)
XLA Modules:
  0.0 93.5 jit_solution(5992252596743766172)
XLA Ops:
  0.0 44.1 %shard_map.109 = (bf16[2,25,64,128]{3,2,1,0:T(8,128)(2,1)}, bf16[4,8,352,128]{3,2,1,0:T(8,128)(2,1)}) custom-call(f32[4]{0:T(128)} %coefficient_ref.1, bf16[25,64,128]{2,1,0:T(8,128)(2,1)} %bitcast.14, bf16[4,640,640]{2,1,0:T(8,128)(2,1)} %refs_0_.1, bf16[4,1024,512]{2,1,0:T(8,128)(2,1)} %bitcast.11, bf16[4,768,384]{2,1,0:T(8,128)(2,1)} %bitcast.13, ...), custom_call_target="tpu_custom_call" | custom-call | tf_op jit(solution)/shard_map/pallas_call | solution.py:201
  44.1 49.4 %shard_map.110 = f32[25,64,128]{2,1,0:T(8,128)} custom-call(s32[48,64]{1,0:T(8,128)} %bitcast.20, s32[1,64]{1,0:T(1,128)} %bitcast.21, bf16[3072,165]{1,0:T(8,128)(2,1)} %bitcast.16, bf16[3072,128]{1,0:T(8,128)(2,1)} %bitcast.18, bf16[25,64,128]{2,1,0:T(8,128)(2,1)} %bitcast.15, bf16[2,25,64,128]{3,2,1,0:T(8,128)(2,1)} %get-tuple-element.7.sides_ref, ...), custom_call_target="tpu_custom_call" | custom-call | tf_op jit(solution)/shard_map/pallas_call | solution.py:463

commit v2 on v1

v2 whole, which is shorter than its diff:
```python
import functools

import jax
import jax.numpy as jnp
import numpy as np
from jax import lax
from jax.experimental import pallas as pl
from jax.experimental.pallas import tpu as pltpu
from jax.sharding import PartitionSpec as P

DEGREES = 5
COMPONENTS = DEGREES * DEGREES
AXES = ("wide", "narrow")
MESH = pl.DeviceIdType.MESH
PLAN = (2, 5, 8, 10, 13, 18, 23)


def flat_rows(weights):
    return weights.reshape(weights.shape[0], -1, weights.shape[-1])


def remote(src, dst, send, recv, device):
    return pltpu.make_async_remote_copy(
        src_ref=src,
        dst_ref=dst,
        send_sem=send,
        recv_sem=recv,
        device_id=device,
        device_id_type=MESH,
    )


def spans():
    return [(degree, degree * degree, 2 * degree + 1) for degree in reversed(range(DEGREES))]


def iota(shape, axis):
    return lax.broadcasted_iota(jnp.int32, shape, axis)


def eye(rows, columns):
    return (iota((rows, columns), 0) == iota((rows, columns), 1)).astype(jnp.bfloat16)


ACROSS = (((1,), (1,)), ((), ()))


def exchange_kernel(sizes, plan, coefficient_ref, neighbours_ref, *refs):
    wide, narrow, count = sizes
    features_ref, frames_ref, radial_ref = refs[:3]
    refs = refs[3:]
    stacks = refs[:count]
    turned_ref, merged_ref = refs[count : count + 2]
    staged = refs[count + 2 : 2 * count + 2]
    (
        partial_ref,
        received_ref,
        share_ref,
        extended_ref,
        upright_ref,
        frames_v,
        radial_v,
        rows_ref,
        picked_ref,
        frame_t,
        radial_t,
        source_ref,
        spread_ref,
        kept_ref,
        load_sem,
        own_sem,
        halo_send,
        halo_recv,
        send_sem,
        recv_sem,
        line_send,
        line_recv,
        plane_send,
        plane_recv,
        pair_send,
        pair_recv,
        local_sem,
        turned_sem,
    ) = refs[2 * count + 2 :]
    my_wide = lax.axis_index("wide")
    my_narrow = lax.axis_index("narrow")
    part = partial_ref.shape[0] // wide
    chips = wide // 2
    my_chip = my_wide // 2
    my_core = lax.rem(my_wide, 2)
    slots, atoms = neighbours_ref.shape
    blocks, _, lanes = picked_ref.shape
    entries = frames_v.shape[1]
    channels = radial_v.shape[1]
    extended = extended_ref.shape[1]

    loads = []
    for at, (stack, stage) in enumerate(zip(stacks, staged)):
        rows = stage.shape[1]
        loads.append(
            pltpu.make_async_copy(
                stack.at[:, pl.ds(pl.multiple_of(my_narrow * rows, 16), rows), :],
                stage,
                load_sem.at[at],
            )
        )
        loads[-1].start()
    own = [
        pltpu.make_async_copy(features_ref, extended_ref.at[:, pl.ds(atoms, atoms), :], own_sem.at[0]),
        pltpu.make_async_copy(frames_ref, frames_v, own_sem.at[1]),
        pltpu.make_async_copy(radial_ref, radial_v, own_sem.at[2]),
    ]
    for copy in own:
        copy.start()

    total = wide * narrow
    me = my_wide * narrow + my_narrow
    after = lax.rem(me + 1, total)
    before = lax.rem(me + total - 1, total)
    place = lambda flat: (flat // narrow, lax.rem(flat, narrow))
    peers = [(lax.rem(my_wide + hop, wide), my_narrow) for hop in range(1, wide)]
    line = [(my_wide, lax.rem(my_narrow + hop, narrow)) for hop in range(1, narrow)]
    greeted = [place(after), place(before)] + peers + line
    barrier = pltpu.get_barrier_semaphore()
    for device in greeted:
        pl.semaphore_signal(barrier, inc=1, device_id=device, device_id_type=MESH)
    pl.semaphore_wait(barrier, len(greeted))

    halo = []
    for at, (degree, base, size) in enumerate(spans()):
        for side, device in enumerate([place(after), place(before)]):
            halo.append(
                remote(
                    features_ref.at[pl.ds(base, size)],
                    extended_ref.at[pl.ds(base, size), pl.ds(2 * side * atoms, atoms), :],
                    halo_send.at[2 * at + side],
                    halo_recv.at[2 * at + side],
                    device,
                )
            )
            halo[-1].start()

    offset = 0
    for load, stage in zip(loads, staged):
        load.wait()
        experts, rows, columns = stage.shape
        for block in range(columns // 128):
            lane = pl.ds(block * 128, 128)
            value = coefficient_ref[0] * stage[0, :, lane].astype(jnp.float32)
            for expert in range(1, experts):
                value = value + coefficient_ref[expert] * stage[expert, :, lane].astype(
                    jnp.float32
                )
            partial_ref[pl.ds(offset, rows), :] = value.astype(jnp.bfloat16)
            offset += rows
    if offset < partial_ref.shape[0]:
        rest = partial_ref.shape[0] - offset
        partial_ref[pl.ds(offset, rest), :] = jnp.zeros((rest, 128), jnp.bfloat16)

    scatter = []
    for hop, device in enumerate(peers):
        target = device[0]
        scatter.append(
            remote(
                partial_ref.at[pl.ds(pl.multiple_of(target * part, 16), part), :],
                received_ref.at[hop],
                send_sem.at[hop],
                recv_sem.at[hop],
                device,
            )
        )
        scatter[-1].start()

    everything = atoms * total
    relative = neighbours_ref[...] - (me * atoms - atoms)
    relative = jnp.where(relative < 0, relative + everything, relative)
    relative = jnp.where(relative >= everything, relative - everything, relative)
    relative = jnp.minimum(relative, 255)
    rows_ref[...] = relative.astype(jnp.float32).astype(jnp.bfloat16)
    for copy in own:
        copy.wait()

    def prepare(b, carried):
        edge = iota((1, lanes), 1) + b * lanes
        home = edge // slots
        slot = edge - home * slots
        chosen = (iota((atoms, lanes), 0) == home).astype(jnp.bfloat16)
        spread = jnp.dot(rows_ref[...], chosen, preferred_element_type=jnp.float32)
        index = jnp.sum(
            jnp.where(iota((slots, lanes), 0) == slot, spread, 0.0), axis=0, keepdims=True
        ).astype(jnp.int32)
        picked_ref[b] = (iota((extended, lanes), 0) == index).astype(jnp.bfloat16)
        row = pl.ds(pl.multiple_of(b * lanes, lanes), lanes)
        frame_t[b] = lax.dot_general(
            eye(frame_t.shape[1], entries),
            frames_v[row, :],
            ACROSS,
            preferred_element_type=jnp.float32,
        )
        radial_t[b] = lax.dot_general(
            eye(channels, channels), radial_v[row, :], ACROSS, preferred_element_type=jnp.float32
        ).astype(jnp.bfloat16)
        return carried

    lax.fori_loop(0, blocks, prepare, 0)

    summed = partial_ref[pl.ds(pl.multiple_of(my_wide * part, 16), part), :].astype(jnp.float32)
    for hop in range(wide - 1):
        scatter[hop].wait_recv()
        summed = summed + received_ref[hop].astype(jnp.float32)
    share_ref[...] = summed.astype(jnp.bfloat16)

    keep = pltpu.make_async_copy(share_ref, merged_ref.at[my_narrow, my_wide], local_sem)
    keep.start()
    partner = (my_wide + 1 - 2 * my_core, my_narrow)
    origin = lambda hop: lax.rem(my_narrow + narrow - hop, narrow)

    def line_copy(hop):
        return remote(
            share_ref,
            merged_ref.at[my_narrow, my_wide],
            line_send.at[hop - 1],
            line_recv.at[hop - 1],
            line[hop - 1],
        )

    def plane_copy(hop, step):
        slot = merged_ref.at[origin(hop), my_wide]
        at = hop * (chips - 1) + step - 1
        target = lax.rem(my_chip + step, chips) * 2 + my_core
        return remote(
            share_ref if hop == 0 else slot,
            slot,
            plane_send.at[at],
            plane_recv.at[at],
            (target, my_narrow),
        )

    def pair_copy(hop, step):
        owner = lax.rem(my_chip + chips - step, chips) * 2 + my_core
        slot = merged_ref.at[origin(hop), owner]
        at = hop * chips + step
        source = share_ref if hop == 0 and step == 0 else slot
        return remote(source, slot, pair_send.at[at], pair_recv.at[at], partner)

    def forward(hop):
        if hop:
            line_copy(hop).wait_recv()
        for step in range(1, chips):
            plane_copy(hop, step).start()
        pair_copy(hop, 0).start()

    def relay(hop):
        for step in range(1, chips):
            plane_copy(hop, step).wait_recv()
            pair_copy(hop, step).start()

    for hop in range(1, narrow):
        line_copy(hop).start()
    forward(0)

    steps = [functools.partial(forward, hop) for hop in range(1, narrow)]
    steps += [functools.partial(relay, hop) for hop in range(narrow)]
    ticks = dict(zip(plan, steps))
    rest = steps[len(plan) :]

    height = spread_ref.shape[1]
    for at, (degree, base, size) in enumerate(spans()):
        for side in range(2):
            halo[2 * at + side].wait_recv()
        for component in range(base, base + size):
            upright_ref[pl.ds(component * channels, channels), :] = jnp.transpose(
                extended_ref[component]
            )
        tall = pl.ds(base * channels, size * channels)
        first = sum((2 * d + 1) ** 2 for d in range(degree))

        def rotate(b, carried):
            for block, step in ticks.items():
                if block // blocks == at:
                    pl.when(b == block % blocks)(step)
            for q in range(size):
                source_ref[pl.ds(q * channels, channels), :] = jnp.dot(
                    upright_ref[pl.ds((base + q) * channels, channels), :],
                    picked_ref[b],
                    preferred_element_type=jnp.float32,
                ).astype(jnp.bfloat16)
            for k in range(size * size):
                row = frame_t[b, pl.ds(first + k, 1), :]
                spread_ref[k] = jnp.broadcast_to(row, spread_ref.shape[1:]).astype(jnp.bfloat16)
            for row in range(0, channels, height):
                scale = radial_t[b, pl.ds(row, height), :]
                xs = [source_ref[pl.ds(q * channels + row, height), :] for q in range(size)]
                for p in range(size):
                    value = spread_ref[p * size] * xs[0]
                    for q in range(1, size):
                        value = value + spread_ref[p * size + q] * xs[q]
                    kept_ref[b, pl.ds((base + p) * channels + row, height), :] = value * scale
            pltpu.make_async_copy(
                kept_ref.at[b, tall, :], turned_ref.at[b, tall, :], turned_sem.at[b, at]
            ).start()
            return carried

        lax.fori_loop(0, blocks, rotate, 0)

    for step in rest:
        step()
    for hop in range(narrow):
        for step in range(chips):
            pair_copy(hop, step).wait_recv()
    for hop in range(1, narrow):
        line_copy(hop).wait_send()
    for hop in range(narrow):
        for step in range(chips):
            pair_copy(hop, step).wait_send()
            if step:
                plane_copy(hop, step).wait_send()
    for copy in scatter + halo:
        copy.wait_send()
    keep.wait()
    for at, (degree, base, size) in enumerate(spans()):
        tall = pl.ds(base * channels, size * channels)
        for b in range(blocks):
            pltpu.make_async_copy(
                kept_ref.at[b, tall, :], turned_ref.at[b, tall, :], turned_sem.at[b, at]
            ).wait()


def exchange(features, frames, radial, neighbours, coefficients, stacks, lanes, plan):
    wide = lax.axis_size("wide")
    narrow = lax.axis_size("narrow")
    stacks = [flat_rows(w) for w in stacks]
    staged = [(w.shape[0], w.shape[1] // narrow, w.shape[2]) for w in stacks]
    rows = sum(shape[1] * shape[2] // 128 for shape in staged)
    unit = 16 * wide
    rows = -(-rows // unit) * unit
    part = rows // wide
    chips = wide // 2
    components, atoms, channels = features.shape
    edges, entries = frames.shape
    blocks = edges // lanes
    padded = -(-entries // 16) * 16
    height = 16
    anywhere = pl.BlockSpec(memory_space=pl.ANY)
    dma = lambda *n: pltpu.SemaphoreType.DMA(n)
    bf16 = lambda *shape: pltpu.VMEM(shape, jnp.bfloat16)
    widest = 2 * DEGREES - 1
    return pl.pallas_call(
        functools.partial(exchange_kernel, (wide, narrow, len(stacks)), plan),
        in_specs=[
            pl.BlockSpec(memory_space=pltpu.SMEM),
            pl.BlockSpec(memory_space=pltpu.VMEM),
        ]
        + [anywhere] * (3 + len(stacks)),
        out_specs=[anywhere, anywhere],
        out_shape=[
            jax.ShapeDtypeStruct((blocks, components * channels, lanes), jnp.bfloat16),
            jax.ShapeDtypeStruct((narrow, wide, part, 128), jnp.bfloat16),
        ],
        scratch_shapes=[bf16(*shape) for shape in staged]
        + [
            bf16(rows, 128),
            bf16(wide - 1, part, 128),
            bf16(part, 128),
            bf16(components, 3 * atoms, channels),
            bf16(components * channels, 3 * atoms),
            bf16(edges, entries),
            bf16(edges, channels),
            bf16(neighbours.shape[0], atoms),
            bf16(blocks, 3 * atoms, lanes),
            pltpu.VMEM((blocks, padded, lanes), jnp.float32),
            bf16(blocks, channels, lanes),
            bf16(widest * channels, lanes),
            bf16(widest * widest, height, lanes),
            bf16(blocks, components * channels, lanes),
            dma(len(stacks)),
            dma(3),
            dma(2 * DEGREES),
            dma(2 * DEGREES),
            dma(wide - 1),
            dma(wide - 1),
            dma(narrow - 1),
            dma(narrow - 1),
            dma(narrow * (chips - 1)),
            dma(narrow * (chips - 1)),
            dma(narrow * chips),
            dma(narrow * chips),
            pltpu.SemaphoreType.DMA,
            dma(blocks, DEGREES),
        ],
        compiler_params=pltpu.CompilerParams(
            collective_id=0, has_side_effects=True, vmem_limit_bytes=60 * 1024 * 1024
        ),
    )(coefficients, neighbours, features, frames, radial, *stacks)


def convolve_kernel(
    shapes,
    slots,
    counts_ref,
    frames_ref,
    turned_ref,
    merged_ref,
    out_ref,
    frame_ref,
    gated_ref,
    total_ref,
    column_ref,
    *weight_refs,
):
    step = pl.program_id(0)
    components, atoms, channels = out_ref.shape
    lanes, entries = frames_ref.shape
    members = merged_ref.shape[0]

    @pl.when(step == 0)
    def _():
        total_ref[...] = jnp.zeros_like(total_ref)
        square = (atoms, atoms)
        diagonal = iota(square, 0) == iota(square, 1)
        count = jnp.sum(
            jnp.where(diagonal, counts_ref[...].astype(jnp.float32), 0.0), axis=1, keepdims=True
        )
        column_ref[...] = jnp.broadcast_to(count, column_ref.shape)
        offset = 0
        for weight_ref, (rows, columns) in zip(weight_refs, shapes):
            part = rows // members
            for block in range(columns // 128):
                whole = jnp.concatenate(
                    [merged_ref[m, pl.ds(offset, part), :] for m in range(members)], axis=0
                )
                weight_ref[pl.ds(block * 128, 128), :] = jnp.transpose(whole)
                offset += part

    frame_ref[...] = lax.dot_general(
        eye(frame_ref.shape[0], entries),
        frames_ref[...],
        ACROSS,
        preferred_element_type=jnp.float32,
    )

    component_of = lambda degree, order: degree * degree + degree + order
    rows_of = lambda component: pl.ds(component * channels, channels)
    gather = lambda order: jnp.concatenate(
        [
            turned_ref[0, rows_of(component_of(degree, order)), :]
            for degree in range(abs(order), DEGREES)
        ],
        axis=0,
    )
    central = jnp.dot(weight_refs[0][...], gather(0), preferred_element_type=jnp.float32)
    gate = 1.0 / (1.0 + jnp.exp(-central[:channels]))
    for degree in range(DEGREES):
        gated_ref[rows_of(component_of(degree, 0)), :] = (
            central[degree * channels : (degree + 1) * channels] * gate
        ).astype(jnp.bfloat16)
    for order in range(1, DEGREES):
        plus = gather(order)
        minus = gather(-order)
        for side in range(2):
            pair = [plus, -minus] if side == 0 else [minus, plus]
            mixed = jnp.dot(
                weight_refs[order][...],
                jnp.concatenate(pair, axis=0),
                preferred_element_type=jnp.float32,
            )
            for column, degree in enumerate(range(order, DEGREES)):
                component = component_of(degree, order if side == 0 else -order)
                gated_ref[rows_of(component), :] = (
                    mixed[column * channels : (column + 1) * channels] * gate
                ).astype(jnp.bfloat16)

    edge = iota((1, lanes), 1) + step * lanes
    home = edge // slots
    slot = edge - home * slots
    window = 8
    first = jnp.minimum((step * lanes) // slots, atoms - window)
    position = slot + slots * (home - first) - slots * iota((window, lanes), 0)
    count = column_ref[pl.ds(first, window), :]
    count = jnp.concatenate([count] * (lanes // channels), axis=1)
    live = jnp.where(
        (position >= 0) & (position.astype(jnp.float32) < count) & (position < slots), 1.0, 0.0
    )
    offset = 0
    for degree in range(DEGREES):
        size = 2 * degree + 1
        summed = None
        for q in range(size):
            left = jnp.concatenate(
                [
                    jnp.broadcast_to(frame_ref[pl.ds(offset + q * size + p, 1), :], live.shape) * live
                    for p in range(size)
                ],
                axis=0,
            ).astype(jnp.bfloat16)
            term = lax.dot_general(
                left,
                gated_ref[rows_of(degree * degree + q), :],
                ACROSS,
                preferred_element_type=jnp.float32,
            )
            summed = term if summed is None else summed + term
        for p in range(size):
            at = degree * degree + p
            total_ref[at, pl.ds(first, window), :] = (
                total_ref[at, pl.ds(first, window), :] + summed[p * window : (p + 1) * window]
            )
        offset += size * size

    @pl.when(step == pl.num_programs(0) - 1)
    def _():
        scale = 1.0 / jnp.sqrt(column_ref[...])
        for component in range(components):
            out_ref[component] = total_ref[component] * scale


def body(
    node_features,
    frames,
    radial,
    neighbours,
    counts,
    coefficients,
    w_zero,
    w_one,
    w_two,
    w_three,
    w_four,
):
    atoms, components, channels = node_features.shape
    slots = neighbours.shape[1]
    entries = frames.shape[2]
    edges = atoms * slots
    stacks = (w_zero, w_one, w_two, w_three, w_four)
    lanes = 256
    features = node_features.transpose(1, 0, 2)
    frames = frames.reshape(edges, entries)
    turned, merged = exchange(
        features,
        frames,
        radial.reshape(edges, channels),
        neighbours.T,
        coefficients,
        stacks,
        lanes,
        PLAN,
    )
    merged = merged.reshape(merged.shape[0], -1, 128)
    shapes = [(int(np.prod(w.shape[1:-1])), w.shape[-1]) for w in stacks]

    padded = -(-entries // 16) * 16
    whole = lambda shape: pl.BlockSpec(shape, lambda i: (0,) * len(shape))
    out = pl.pallas_call(
        functools.partial(convolve_kernel, shapes, slots),
        grid=(edges // lanes,),
        in_specs=[
            whole((1, atoms)),
            pl.BlockSpec((lanes, entries), lambda i: (i, 0)),
            pl.BlockSpec((1, components * channels, lanes), lambda i: (i, 0, 0)),
            whole(merged.shape),
        ],
        out_specs=whole((components, atoms, channels)),
        out_shape=jax.ShapeDtypeStruct((components, atoms, channels), jnp.float32),
        scratch_shapes=[
            pltpu.VMEM((padded, lanes), jnp.float32),
            pltpu.VMEM((components * channels, lanes), jnp.bfloat16),
            pltpu.VMEM((components, atoms, channels), jnp.float32),
            pltpu.VMEM((atoms, channels), jnp.float32),
        ]
        + [pltpu.VMEM((n, k), jnp.bfloat16) for k, n in shapes],
        compiler_params=pltpu.CompilerParams(
            dimension_semantics=("arbitrary",), vmem_limit_bytes=56 * 1024 * 1024
        ),
    )(counts.reshape(1, atoms), frames, turned, merged)
    return out.transpose(1, 0, 2)


def solution(mesh):
    spread = lambda rest: P(AXES, *([None] * rest))
    in_specs = (
        spread(2),
        spread(2),
        spread(2),
        spread(1),
        spread(0),
        P("wide"),
        P("wide", None, None),
        P("wide", None, None, None),
        P("wide", None, None, None),
        P("wide", None, None, None),
        P("wide", None, None, None),
    )
    return jax.shard_map(body, mesh=mesh, in_specs=in_specs, out_specs=spread(2), check_vma=False)
```

time: 93.6 us -> 83.2 us (0.89)
  Pallas kernels: 93.5 us -> 83 us
    pallas_call x1, Pallas kernels: 49.4 us -> 27.2 us  [body(): pl.pallas_call(functools.partial(convolve_kernel, shapes, slots), grid=(e...]
    pallas_call x1, Pallas kernels: 44.1 us -> 55.8 us  [exchange(): pl.pallas_call(functools.partial(exchange_kernel, (wide, narrow, len(stac...]
where the time goes in v2:
time: 83.2 us; the launch traced here: 83 us
  Pallas kernels  83 us (100%)
    pallas_call x1, Pallas kernels, exchange(): pl.pallas_call(functools.partial(exchange_kernel, (wide, narrow, len(stac...  55.8 us
    pallas_call x1, Pallas kernels, body(): pl.pallas_call(functools.partial(convolve_kernel, shapes, slots), grid=(e...  27.2 us

profile of v2, /device:TPU:0, one launch (start us, length us, event | category | flops | bytes accessed | tf_op | source)
XLA Modules:
  0.0 83.0 jit_solution(12519718540410832016)
XLA Ops:
  0.0 55.8 %shard_map.109 = (bf16[12,3200,256]{2,1,0:T(8,128)(2,1)}, bf16[4,8,352,128]{3,2,1,0:T(8,128)(2,1)}) custom-call(f32[4]{0:T(128)} %coefficient_ref.1, s32[48,64]{1,0:T(8,128)} %bitcast.20, bf16[25,64,128]{2,1,0:T(8,128)(2,1)} %bitcast.18, bf16[3072,165]{1,0:T(8,128)(2,1)} %bitcast.11, bf16[3072,128]{1,0:T(8,128)(2,1)} %bitcast.17, ...), custom_call_target="tpu_custom_call" | custom-call | tf_op jit(solution)/shard_map/pallas_call | solution.py:348
  55.8 27.2 %shard_map.110 = f32[25,64,128]{2,1,0:T(8,128)} custom-call(s32[1,64]{1,0:T(1,128)} %bitcast.21, bf16[3072,165]{1,0:T(8,128)(2,1)} %bitcast.12, bf16[12,3200,256]{2,1,0:T(8,128)(2,1)} %get-tuple-element.7.turned_ref, bf16[4,2816,128]{2,1,0:T(8,128)(2,1)} %bitcast.14), custom_call_target="tpu_custom_call" | custom-call | tf_op jit(solution)/shard_map/pallas_call | solution.py:553

commit v3 on v2

v3 whole, which is shorter than its diff:
```python
import functools

import jax
import jax.numpy as jnp
import numpy as np
from jax import lax
from jax.experimental import pallas as pl
from jax.experimental.pallas import tpu as pltpu
from jax.sharding import PartitionSpec as P

DEGREES = 5
COMPONENTS = DEGREES * DEGREES
AXES = ("wide", "narrow")
MESH = pl.DeviceIdType.MESH
EARLY = 2
PLAN = (8, 10, 16, 20, 22, 24, 28, 32, 36, 40, 44)


def flat_rows(weights):
    return weights.reshape(weights.shape[0], -1, weights.shape[-1])


def remote(src, dst, send, recv, device):
    return pltpu.make_async_remote_copy(
        src_ref=src,
        dst_ref=dst,
        send_sem=send,
        recv_sem=recv,
        device_id=device,
        device_id_type=MESH,
    )


def spans():
    return [(degree, degree * degree, 2 * degree + 1) for degree in reversed(range(DEGREES))]


def iota(shape, axis):
    return lax.broadcasted_iota(jnp.int32, shape, axis)


def eye(rows, columns):
    return (iota((rows, columns), 0) == iota((rows, columns), 1)).astype(jnp.bfloat16)


ACROSS = (((1,), (1,)), ((), ()))


def whole_kernel(sizes, shapes, plan, coefficient_ref, neighbours_ref, counts_ref, *refs):
    wide, narrow, count = sizes
    features_ref, frames_ref, radial_ref = refs[:3]
    refs = refs[3:]
    stacks = refs[:count]
    out_ref = refs[count]
    staged = refs[count + 1 : 2 * count + 1]
    weight_refs = refs[2 * count + 1 : 3 * count + 1]
    (
        partial_ref,
        received_ref,
        paired_ref,
        chip_ref,
        share_ref,
        extended_ref,
        upright_ref,
        frames_v,
        radial_v,
        rows_ref,
        picked_ref,
        frame_t,
        radial_t,
        source_ref,
        source_b,
        kept_ref,
        merged_ref,
        gated_ref,
        total_ref,
        column_ref,
        load_sem,
        own_sem,
        halo_send,
        halo_recv,
        send_sem,
        recv_sem,
        line_send,
        line_recv,
        plane_send,
        plane_recv,
        cross_send,
        cross_recv,
        pair_send,
        pair_recv,
        local_sem,
    ) = refs[3 * count + 1 :]
    my_wide = lax.axis_index("wide")
    my_narrow = lax.axis_index("narrow")
    part = partial_ref.shape[0] // wide
    chips = wide // 2
    my_chip = my_wide // 2
    my_core = lax.rem(my_wide, 2)
    slots, atoms = neighbours_ref.shape
    blocks, _, lanes = picked_ref.shape
    entries = frames_v.shape[1]
    channels = radial_v.shape[1]
    extended = extended_ref.shape[1]

    loads = []
    for at, (stack, stage) in enumerate(zip(stacks, staged)):
        rows = stage.shape[1]
        loads.append(
            pltpu.make_async_copy(
                stack.at[:, pl.ds(pl.multiple_of(my_narrow * rows, 16), rows), :],
                stage,
                load_sem.at[at],
            )
        )
        loads[-1].start()
    own = [
        pltpu.make_async_copy(features_ref, extended_ref.at[:, pl.ds(atoms, atoms), :], own_sem.at[0]),
        pltpu.make_async_copy(frames_ref, frames_v, own_sem.at[1]),
        pltpu.make_async_copy(radial_ref, radial_v, own_sem.at[2]),
    ]
    for copy in own:
        copy.start()

    total = wide * narrow
    me = my_wide * narrow + my_narrow
    after = lax.rem(me + 1, total)
    before = lax.rem(me + total - 1, total)
    place = lambda flat: (flat // narrow, lax.rem(flat, narrow))
    partner = (my_wide + 1 - 2 * my_core, my_narrow)
    peers = [
        (lax.rem(my_chip + hop, chips) * 2 + my_core, my_narrow) for hop in range(1, chips)
    ] + [partner]
    line = [(my_wide, lax.rem(my_narrow + hop, narrow)) for hop in range(1, narrow)]
    greeted = [place(after), place(before)] + peers + line
    barrier = pltpu.get_barrier_semaphore()
    for device in greeted:
        pl.semaphore_signal(barrier, inc=1, device_id=device, device_id_type=MESH)
    pl.semaphore_wait(barrier, len(greeted))

    def halo_copy(at, side):
        degree, base, size = spans()[at]
        return remote(
            features_ref.at[pl.ds(base, size)],
            extended_ref.at[pl.ds(base, size), pl.ds(2 * side * atoms, atoms), :],
            halo_send.at[2 * at + side],
            halo_recv.at[2 * at + side],
            [place(after), place(before)][side],
        )

    for at in range(EARLY):
        for side in range(2):
            halo_copy(at, side).start()

    offset = 0
    for load, stage in zip(loads, staged):
        load.wait()
        experts, rows, columns = stage.shape
        for block in range(columns // 128):
            lane = pl.ds(block * 128, 128)
            value = coefficient_ref[0] * stage[0, :, lane].astype(jnp.float32)
            for expert in range(1, experts):
                value = value + coefficient_ref[expert] * stage[expert, :, lane].astype(
                    jnp.float32
                )
            partial_ref[pl.ds(offset, rows), :] = value.astype(jnp.bfloat16)
            offset += rows
    if offset < partial_ref.shape[0]:
        rest = partial_ref.shape[0] - offset
        partial_ref[pl.ds(offset, rest), :] = jnp.zeros((rest, 128), jnp.bfloat16)

    half = chips * part
    theirs = pl.ds(pl.multiple_of((1 - my_core) * half, 16), half)
    pairing = remote(
        partial_ref.at[theirs, :], paired_ref, send_sem.at[0], recv_sem.at[0], partner
    )
    pairing.start()

    everything = atoms * total
    relative = neighbours_ref[...] - (me * atoms - atoms)
    relative = jnp.where(relative < 0, relative + everything, relative)
    relative = jnp.where(relative >= everything, relative - everything, relative)
    relative = jnp.minimum(relative, 255)
    rows_ref[...] = relative.astype(jnp.float32).astype(jnp.bfloat16)
    for copy in own:
        copy.wait()

    def prepare(b, carried):
        edge = iota((1, lanes), 1) + b * lanes
        home = edge // slots
        slot = edge - home * slots
        chosen = (iota((atoms, lanes), 0) == home).astype(jnp.bfloat16)
        spread = jnp.dot(rows_ref[...], chosen, preferred_element_type=jnp.float32)
        index = jnp.sum(
            jnp.where(iota((slots, lanes), 0) == slot, spread, 0.0), axis=0, keepdims=True
        ).astype(jnp.int32)
        picked_ref[b] = (iota((extended, lanes), 0) == index).astype(jnp.bfloat16)
        row = pl.ds(pl.multiple_of(b * lanes, lanes), lanes)
        frame_t[b] = lax.dot_general(
            eye(frame_t.shape[1], entries),
            frames_v[row, :],
            ACROSS,
            preferred_element_type=jnp.float32,
        )
        scales = lax.dot_general(
            eye(channels, channels), radial_v[row, :], ACROSS, preferred_element_type=jnp.float32
        ).astype(jnp.bfloat16)
        radial_t[b] = scales.reshape(radial_t.shape[1:])
        return carried

    lax.fori_loop(0, blocks // 4, prepare, 0)

    pairing.wait_recv()
    scatter = []
    for hop in range(1, chips):
        target = lax.rem(my_chip + hop, chips)
        mine = pl.ds(pl.multiple_of(my_core * half + target * part, 16), part)
        there = pl.ds(pl.multiple_of(target * part, 16), part)
        chip_ref[hop - 1] = (
            partial_ref[mine, :].astype(jnp.float32) + paired_ref[there, :].astype(jnp.float32)
        ).astype(jnp.bfloat16)
        scatter.append(
            remote(
                chip_ref.at[hop - 1],
                received_ref.at[hop - 1],
                send_sem.at[hop],
                recv_sem.at[hop],
                (target * 2 + my_core, my_narrow),
            )
        )
        scatter[-1].start()
    lax.fori_loop(blocks // 4, blocks, prepare, 0)
    mine = pl.ds(pl.multiple_of(my_core * half + my_chip * part, 16), part)
    there = pl.ds(pl.multiple_of(my_chip * part, 16), part)
    summed = partial_ref[mine, :].astype(jnp.float32) + paired_ref[there, :].astype(jnp.float32)
    for hop in range(chips - 1):
        scatter[hop].wait_recv()
        summed = summed + received_ref[hop].astype(jnp.float32)
    share_ref[...] = summed.astype(jnp.bfloat16)

    my_place = my_core * chips + my_chip
    keep = pltpu.make_async_copy(share_ref, merged_ref.at[my_narrow, pl.ds(pl.multiple_of(my_place * part, 16), part), :], local_sem)
    keep.start()
    origin = lambda hop: lax.rem(my_narrow + narrow - hop, narrow)

    square = chips == 4
    if square:
        hops = [my_chip + 1 - 2 * lax.rem(my_chip, 2), my_chip + 2 - 4 * (my_chip // 2)]
        far = lax.rem(my_chip + 1, 2) + 2 * (1 - my_chip // 2)
        sources = hops
        owners = [my_chip] + hops + [far]
    else:
        hops = [lax.rem(my_chip + step, chips) for step in range(1, chips)]
        sources = [lax.rem(my_chip + chips - step, chips) for step in range(1, chips)]
        owners = [my_chip] + sources

    def spot(hop, chip, start=0, rows=part):
        row = (my_core * chips + chip) * part + start
        return merged_ref.at[origin(hop), pl.ds(pl.multiple_of(row, 16), rows), :]


    def line_copy(hop):
        return remote(
            share_ref,
            merged_ref.at[my_narrow, pl.ds(pl.multiple_of(my_place * part, 16), part), :],
            line_send.at[hop - 1],
            line_recv.at[hop - 1],
            line[hop - 1],
        )

    def plane_copy(hop, way):
        slot = spot(hop, my_chip)
        at = hop * len(hops) + way
        return remote(
            share_ref if hop == 0 else slot,
            slot,
            plane_send.at[at],
            plane_recv.at[at],
            (hops[way] * 2 + my_core, my_narrow),
        )

    def cross_copy(hop, way):
        slot = spot(hop, hops[way], way * cut, cut if way == 0 else part - cut)
        at = hop * 2 + way
        return remote(
            slot,
            slot,
            cross_send.at[at],
            cross_recv.at[at],
            (hops[1 - way] * 2 + my_core, my_narrow),
        )

    cut = part // 32 * 16

    def crossed(hop, way):
        slot = spot(hop, far, way * cut, cut if way == 0 else part - cut)
        at = hop * 2 + way
        return remote(
            slot,
            slot,
            cross_send.at[at],
            cross_recv.at[at],
            (hops[1 - way] * 2 + my_core, my_narrow),
        )

    def pair_copy(hop, step):
        slot = spot(hop, owners[step])
        at = hop * chips + step
        source = share_ref if hop == 0 and step == 0 else slot
        return remote(source, slot, pair_send.at[at], pair_recv.at[at], partner)

    def forward(hop):
        if hop:
            line_copy(hop).wait_recv()
        for way in range(len(hops)):
            plane_copy(hop, way).start()
        pair_copy(hop, 0).start()

    def relay(hop):
        for way in range(len(hops)):
            plane_copy(hop, way).wait_recv()
            if square:
                cross_copy(hop, way).start()
            pair_copy(hop, way + 1).start()

    def close(hop):
        for way in range(2):
            crossed(hop, way).wait_recv()
        pair_copy(hop, 3).start()

    for hop in range(1, narrow):
        line_copy(hop).start()
    for at in range(EARLY, DEGREES):
        for side in range(2):
            halo_copy(at, side).start()
    forward(0)

    steps = []
    for turn in range(narrow + 2):
        if 0 < turn < narrow:
            steps.append(functools.partial(forward, turn))
        if 0 < turn <= narrow:
            steps.append(functools.partial(relay, turn - 1))
        if square and turn > 1:
            steps.append(functools.partial(close, turn - 2))
    ticks = dict(zip(plan, steps))
    rest = steps[len(plan) :]

    groups, height = radial_t.shape[1:3]
    for at, (degree, base, size) in enumerate(spans()):
        for side in range(2):
            halo_copy(at, side).wait_recv()
        for component in range(base, base + size):
            upright_ref[component] = jnp.transpose(extended_ref[component]).reshape(
                upright_ref.shape[1:]
            )
        first = sum((2 * d + 1) ** 2 for d in range(degree))

        def fetch(b, group, source):
            left = jnp.concatenate(
                [upright_ref[base + q, group] for q in range(size)], axis=0
            )
            got = jnp.dot(left, picked_ref[b], preferred_element_type=jnp.float32)
            for q in range(size):
                source[q, group] = got[q * height : (q + 1) * height].astype(jnp.bfloat16)

        def rotate(b, group, source):
            for lane in range(0, lanes, 128):
                part_of = pl.ds(lane, 128)

                def entry(k):
                    row = frame_t[b, pl.ds(first + k, 1), part_of]
                    row = jnp.broadcast_to(row, (16, 128)).astype(jnp.bfloat16)
                    return jnp.concatenate([row] * (height // 16), axis=0)

                scale = radial_t[b, group, :, part_of]
                xs = [source[q, group, :, part_of] for q in range(size)]
                for p in range(size):
                    value = entry(p * size) * xs[0]
                    for q in range(1, size):
                        value = value + entry(p * size + q) * xs[q]
                    kept_ref[b, base + p, group, :, part_of] = value * scale

        def all_groups(work):
            if size > 5:
                lax.fori_loop(0, groups, lambda group, carried: (work(group), carried)[1], 0)
            else:
                for group in range(groups):
                    work(group)

        buffers = [source_ref, source_b]
        all_groups(lambda group: fetch(0, group, buffers[0]))

        def pair(i, carried):
            for block, step in ticks.items():
                if block // blocks == at:
                    pl.when(i == block % blocks // 2)(step)
            for k in range(2):
                b = 2 * i + k
                following = jnp.minimum(b + 1, blocks - 1)

                def both(group, b=b, following=following, k=k):
                    fetch(following, group, buffers[1 - k])
                    rotate(b, group, buffers[k])

                all_groups(both)
            return carried

        lax.fori_loop(0, blocks // 2, pair, 0)

    for step in rest:
        step()
    for hop in range(narrow):
        for step in range(chips):
            pair_copy(hop, step).wait_recv()
    for hop in range(1, narrow):
        line_copy(hop).wait_send()
    for hop in range(narrow):
        for step in range(chips):
            pair_copy(hop, step).wait_send()
        for way in range(len(hops)):
            plane_copy(hop, way).wait_send()
            if square:
                cross_copy(hop, way).wait_send()
    for copy in scatter + [pairing]:
        copy.wait_send()
    for at in range(DEGREES):
        for side in range(2):
            halo_copy(at, side).wait_send()
    keep.wait()

    offset = 0
    for weight_ref, (rows, columns) in zip(weight_refs, shapes):
        piece = rows // narrow
        for block in range(columns // 128):
            gathered = jnp.concatenate(
                [merged_ref[m, pl.ds(offset, piece), :] for m in range(narrow)], axis=0
            )
            weight_ref[pl.ds(block * 128, 128), :] = jnp.transpose(gathered)
            offset += piece
    total_ref[...] = jnp.zeros_like(total_ref)
    square = (atoms, atoms)
    diagonal = iota(square, 0) == iota(square, 1)
    count = jnp.sum(
        jnp.where(diagonal, counts_ref[...].astype(jnp.float32), 0.0), axis=1, keepdims=True
    )
    column_ref[...] = jnp.broadcast_to(count, column_ref.shape)

    def mix(b, carried):
        mix_block(b, slots, kept_ref, frame_t, weight_refs, gated_ref, total_ref, column_ref)
        return carried

    lax.fori_loop(0, blocks, mix, 0)

    scale = 1.0 / jnp.sqrt(column_ref[...])
    for component in range(COMPONENTS):
        out_ref[component] = total_ref[component] * scale


def mix_block(b, slots, kept_ref, frame_t, weight_refs, gated_ref, total_ref, column_ref):
    atoms, channels = column_ref.shape
    lanes = gated_ref.shape[1]
    component_of = lambda degree, order: degree * degree + degree + order
    rows_of = lambda component: pl.ds(component * channels, channels)
    gather = lambda order: jnp.concatenate(
        [
            kept_ref[b, component_of(degree, order)].reshape(channels, lanes)
            for degree in range(abs(order), DEGREES)
        ],
        axis=0,
    )
    central = jnp.dot(weight_refs[0][...], gather(0), preferred_element_type=jnp.float32)
    gate = 1.0 / (1.0 + jnp.exp(-central[:channels]))
    for degree in range(DEGREES):
        gated_ref[rows_of(component_of(degree, 0)), :] = (
            central[degree * channels : (degree + 1) * channels] * gate
        ).astype(jnp.bfloat16)
    for order in range(1, DEGREES):
        plus = gather(order)
        minus = gather(-order)
        for side in range(2):
            pair = [plus, -minus] if side == 0 else [minus, plus]
            mixed = jnp.dot(
                weight_refs[order][...],
                jnp.concatenate(pair, axis=0),
                preferred_element_type=jnp.float32,
            )
            for column, degree in enumerate(range(order, DEGREES)):
                component = component_of(degree, order if side == 0 else -order)
                gated_ref[rows_of(component), :] = (
                    mixed[column * channels : (column + 1) * channels] * gate
                ).astype(jnp.bfloat16)

    edge = iota((1, lanes), 1) + b * lanes
    home = edge // slots
    slot = edge - home * slots
    window = 8
    first = jnp.minimum((b * lanes) // slots, atoms - window)
    position = slot + slots * (home - first) - slots * iota((window, lanes), 0)
    count = column_ref[pl.ds(first, window), :]
    count = jnp.concatenate([count] * (lanes // channels), axis=1)
    live = jnp.where(
        (position >= 0) & (position.astype(jnp.float32) < count) & (position < slots), 1.0, 0.0
    )
    offset = 0
    for degree in range(DEGREES):
        size = 2 * degree + 1
        summed = None
        for q in range(size):
            left = jnp.concatenate(
                [
                    jnp.broadcast_to(frame_t[b, pl.ds(offset + q * size + p, 1), :], live.shape)
                    * live
                    for p in range(size)
                ],
                axis=0,
            ).astype(jnp.bfloat16)
            term = lax.dot_general(
                left,
                gated_ref[rows_of(degree * degree + q), :],
                ACROSS,
                preferred_element_type=jnp.float32,
            )
            summed = term if summed is None else summed + term
        for p in range(size):
            at = degree * degree + p
            total_ref[at, pl.ds(first, window), :] = (
                total_ref[at, pl.ds(first, window), :] + summed[p * window : (p + 1) * window]
            )
        offset += size * size


def run(features, frames, radial, neighbours, counts, coefficients, stacks, lanes, plan):
    shapes = [(int(np.prod(w.shape[1:-1])), w.shape[-1]) for w in stacks]
    wide = lax.axis_size("wide")
    narrow = lax.axis_size("narrow")
    stacks = [flat_rows(w) for w in stacks]
    staged = [(w.shape[0], w.shape[1] // narrow, w.shape[2]) for w in stacks]
    rows = sum(shape[1] * shape[2] // 128 for shape in staged)
    unit = 16 * wide
    rows = -(-rows // unit) * unit
    part = rows // wide
    chips = wide // 2
    components, atoms, channels = features.shape
    edges, entries = frames.shape
    blocks = edges // lanes
    padded = -(-entries // 16) * 16
    groups = 2
    height = channels // groups
    anywhere = pl.BlockSpec(memory_space=pl.ANY)
    vmem = pl.BlockSpec(memory_space=pltpu.VMEM)
    dma = lambda *n: pltpu.SemaphoreType.DMA(n)
    bf16 = lambda *shape: pltpu.VMEM(shape, jnp.bfloat16)
    widest = 2 * DEGREES - 1
    return pl.pallas_call(
        functools.partial(whole_kernel, (wide, narrow, len(stacks)), shapes, plan),
        in_specs=[pl.BlockSpec(memory_space=pltpu.SMEM), vmem, vmem]
        + [anywhere] * (3 + len(stacks)),
        out_specs=vmem,
        out_shape=jax.ShapeDtypeStruct((components, atoms, channels), jnp.float32),
        scratch_shapes=[bf16(*shape) for shape in staged]
        + [bf16(n, k) for k, n in shapes]
        + [
            bf16(rows, 128),
            bf16(chips - 1, part, 128),
            bf16(chips * part, 128),
            bf16(chips - 1, part, 128),
            bf16(part, 128),
            bf16(components, 3 * atoms, channels),
            bf16(components, groups, height, 3 * atoms),
            bf16(edges, entries),
            bf16(edges, channels),
            bf16(neighbours.shape[0], atoms),
            bf16(blocks, 3 * atoms, lanes),
            pltpu.VMEM((blocks, padded, lanes), jnp.float32),
            bf16(blocks, groups, height, lanes),
            bf16(widest, groups, height, lanes),
            bf16(widest, groups, height, lanes),
            bf16(blocks, components, groups, height, lanes),
            bf16(narrow, wide * part, 128),
            bf16(components * channels, lanes),
            pltpu.VMEM((components, atoms, channels), jnp.float32),
            pltpu.VMEM((atoms, channels), jnp.float32),
            dma(len(stacks)),
            dma(3),
            dma(2 * DEGREES),
            dma(2 * DEGREES),
            dma(chips),
            dma(chips),
            dma(narrow - 1),
            dma(narrow - 1),
            dma(narrow * (chips - 1)),
            dma(narrow * (chips - 1)),
            dma(narrow * 2),
            dma(narrow * 2),
            dma(narrow * chips),
            dma(narrow * chips),
            pltpu.SemaphoreType.DMA,
        ],
        compiler_params=pltpu.CompilerParams(
            collective_id=0, has_side_effects=True, vmem_limit_bytes=60 * 1024 * 1024
        ),
    )(coefficients, neighbours, counts, features, frames, radial, *stacks)


def body(
    node_features,
    frames,
    radial,
    neighbours,
    counts,
    coefficients,
    w_zero,
    w_one,
    w_two,
    w_three,
    w_four,
):
    atoms, components, channels = node_features.shape
    slots = neighbours.shape[1]
    entries = frames.shape[2]
    edges = atoms * slots
    stacks = (w_zero, w_one, w_two, w_three, w_four)
    lanes = 256
    features = node_features.transpose(1, 0, 2)
    frames = frames.reshape(edges, entries)
    out = run(
        features,
        frames,
        radial.reshape(edges, channels),
        neighbours.T,
        counts.reshape(1, atoms),
        coefficients,
        stacks,
        lanes,
        PLAN,
    )
    return out.transpose(1, 0, 2)


def solution(mesh):
    spread = lambda rest: P(AXES, *([None] * rest))
    in_specs = (
        spread(2),
        spread(2),
        spread(2),
        spread(1),
        spread(0),
        P("wide"),
        P("wide", None, None),
        P("wide", None, None, None),
        P("wide", None, None, None),
        P("wide", None, None, None),
        P("wide", None, None, None),
    )
    return jax.shard_map(body, mesh=mesh, in_specs=in_specs, out_specs=spread(2), check_vma=False)
```

time: 83.2 us -> 71.6 us (0.86)
  Pallas kernels: 83 us -> 69.3 us
  local copies, waits for them, and re-layouts: 0 us -> 2.12 us
    pallas_call x2 -> x1, Pallas kernels: 83 us -> 69.3 us  [run(): pl.pallas_call(functools.partial(whole_kernel, (wide, narrow, len(stacks)...]
    unnamed x0 -> x1, local copies, waits for them, and re-layouts: none -> 2.12 us
where the time goes in v3:
time: 71.6 us; the launch traced here: 71.4 us
  Pallas kernels  69.3 us (97%)
  local copies, waits for them, and re-layouts  2.12 us (3%)
    pallas_call x1, Pallas kernels, run(): pl.pallas_call(functools.partial(whole_kernel, (wide, narrow, len(stacks)...  69.3 us
    unnamed x1, local copies, waits for them, and re-layouts  2.12 us

profile of v3, /device:TPU:0, one launch (start us, length us, event | category | flops | bytes accessed | tf_op | source)
XLA Modules:
  0.0 71.4 jit_solution(17307094780420904791)
XLA Ops:
  0.0 69.3 %shard_map.109 = f32[25,64,128]{2,1,0:T(8,128)} custom-call(f32[4]{0:T(128)} %coefficient_ref.1, s32[48,64]{1,0:T(8,128)} %bitcast.18, s32[1,64]{1,0:T(1,128)} %bitcast.19, bf16[25,64,128]{2,1,0:T(8,128)(2,1)} %bitcast.16, bf16[3072,165]{1,0:T(8,128)(2,1)} %bitcast.13, bf16[3072,128]{1,0:T(8,128)(2,1)} %bitcast.15, bf16[4,640,640]{2,1,0:T(8,128)(2,1)} %refs_3_.1, ...), custom_call_target="tpu_custom_call" | custom-call | tf_op jit(solution)/shard_map/pallas_call | solution.py:555
  69.3 2.1 %copy.13 = f32[64,25,128]{2,0,1:T(8,128)} copy(f32[64,25,128]{2,0,1:T(8,128)} %bitcast.11) | data formatting | bytes 1638400

commit v4 on v3

--- a/solution.py
+++ b/solution.py
@@ -11,6 +11,7 @@
 DEGREES = 5
 COMPONENTS = DEGREES * DEGREES
 AXES = ("wide", "narrow")
+THREE = (1, 3)
 MESH = pl.DeviceIdType.MESH
 EARLY = 2
 PLAN = (8, 10, 16, 20, 22, 24, 28, 32, 36, 40, 44)
@@ -430,12 +431,18 @@
     keep.wait()
 
     offset = 0
-    for weight_ref, (rows, columns) in zip(weight_refs, shapes):
+    for order, (weight_ref, (rows, columns)) in enumerate(zip(weight_refs, shapes)):
         piece = rows // narrow
         for block in range(columns // 128):
             gathered = jnp.concatenate(
                 [merged_ref[m, pl.ds(offset, piece), :] for m in range(narrow)], axis=0
             )
+            if order in THREE:
+                real = gathered[: rows // 2].astype(jnp.float32)
+                imag = gathered[rows // 2 :].astype(jnp.float32)
+                gathered = jnp.concatenate([real, real + imag, imag - real], axis=0).astype(
+                    jnp.bfloat16
+                )
             weight_ref[pl.ds(block * 128, 128), :] = jnp.transpose(gathered)
             offset += piece
     total_ref[...] = jnp.zeros_like(total_ref)
@@ -478,13 +485,24 @@
     for order in range(1, DEGREES):
         plus = gather(order)
         minus = gather(-order)
+        if order in THREE:
+            deep = plus.shape[0]
+            product = lambda at, right: jnp.dot(
+                weight_refs[order][:, at * deep : (at + 1) * deep],
+                right,
+                preferred_element_type=jnp.float32,
+            )
+            both = product(0, plus + minus)
         for side in range(2):
-            pair = [plus, -minus] if side == 0 else [minus, plus]
-            mixed = jnp.dot(
-                weight_refs[order][...],
-                jnp.concatenate(pair, axis=0),
-                preferred_element_type=jnp.float32,
-            )
+            if order in THREE:
+                mixed = both - product(1, minus) if side == 0 else both + product(2, plus)
+            else:
+                pair = [plus, -minus] if side == 0 else [minus, plus]
+                mixed = jnp.dot(
+                    weight_refs[order][...],
+                    jnp.concatenate(pair, axis=0),
+                    preferred_element_type=jnp.float32,
+                )
             for column, degree in enumerate(range(order, DEGREES)):
                 component = component_of(degree, order if side == 0 else -order)
                 gated_ref[rows_of(component), :] = (
@@ -559,7 +577,7 @@
         out_specs=vmem,
         out_shape=jax.ShapeDtypeStruct((components, atoms, channels), jnp.float32),
         scratch_shapes=[bf16(*shape) for shape in staged]
-        + [bf16(n, k) for k, n in shapes]
+        + [bf16(n, k // 2 * 3 if at in THREE else k) for at, (k, n) in enumerate(shapes)]
         + [
             bf16(rows, 128),
             bf16(chips - 1, part, 128),

time: 71.6 us -> 69.8 us (0.975)
  Pallas kernels: 69.3 us -> 67.5 us
    pallas_call x1, Pallas kernels: 69.3 us -> 67.5 us  [run(): pl.pallas_call(functools.partial(whole_kernel, (wide, narrow, len(stacks)...]
where the time goes in v4:
time: 69.8 us; the launch traced here: 69.6 us
  Pallas kernels  67.5 us (97%)
  local copies, waits for them, and re-layouts  2.12 us (3%)
    pallas_call x1, Pallas kernels, run(): pl.pallas_call(functools.partial(whole_kernel, (wide, narrow, len(stacks)...  67.5 us
    unnamed x1, local copies, waits for them, and re-layouts  2.12 us

profile of v4, /device:TPU:0, one launch (start us, length us, event | category | flops | bytes accessed | tf_op | source)
XLA Modules:
  0.0 69.6 jit_solution(4855560033479620820)
XLA Ops:
  0.0 67.5 %shard_map.109 = f32[25,64,128]{2,1,0:T(8,128)} custom-call(f32[4]{0:T(128)} %coefficient_ref.1, s32[48,64]{1,0:T(8,128)} %bitcast.18, s32[1,64]{1,0:T(1,128)} %bitcast.19, bf16[25,64,128]{2,1,0:T(8,128)(2,1)} %bitcast.16, bf16[3072,165]{1,0:T(8,128)(2,1)} %bitcast.13, bf16[3072,128]{1,0:T(8,128)(2,1)} %bitcast.15, bf16[4,640,640]{2,1,0:T(8,128)(2,1)} %refs_3_.1, ...), custom_call_target="tpu_custom_call" | custom-call | tf_op jit(solution)/shard_map/pallas_call | solution.py:573
  67.5 2.1 %copy.13 = f32[64,25,128]{2,0,1:T(8,128)} copy(f32[64,25,128]{2,0,1:T(8,128)} %bitcast.11) | data formatting | bytes 1638400

commit v5 on v4

--- a/solution.py
+++ b/solution.py
@@ -14,7 +14,7 @@
 THREE = (1, 3)
 MESH = pl.DeviceIdType.MESH
 EARLY = 2
-PLAN = (8, 10, 16, 20, 22, 24, 28, 32, 36, 40, 44)
+PLAN = (8, 10, 18, 22, 24, 28, 34, 38, 42, 48, 54)
 
 
 def flat_rows(weights):
@@ -74,6 +74,7 @@
         kept_ref,
         merged_ref,
         gated_ref,
+        gated_b,
         total_ref,
         column_ref,
         load_sem,
@@ -453,19 +454,29 @@
     )
     column_ref[...] = jnp.broadcast_to(count, column_ref.shape)
 
-    def mix(b, carried):
-        mix_block(b, slots, kept_ref, frame_t, weight_refs, gated_ref, total_ref, column_ref)
+    def mix(b, buffer, beside=lambda: None):
+        mix_block(b, kept_ref, weight_refs, buffer, beside)
+
+    def gather(b, buffer):
+        sum_block(b, slots, frame_t, buffer, total_ref, column_ref)
+
+    def two(i, carried):
+        mix(2 * i + 1, gated_b, lambda: gather(2 * i, gated_ref))
+        mix(2 * i + 2, gated_ref, lambda: gather(2 * i + 1, gated_b))
         return carried
 
-    lax.fori_loop(0, blocks, mix, 0)
+    mix(0, gated_ref)
+    lax.fori_loop(0, blocks // 2 - 1, two, 0)
+    mix(blocks - 1, gated_b, lambda: gather(blocks - 2, gated_ref))
+    gather(blocks - 1, gated_b)
 
     scale = 1.0 / jnp.sqrt(column_ref[...])
     for component in range(COMPONENTS):
         out_ref[component] = total_ref[component] * scale
 
 
-def mix_block(b, slots, kept_ref, frame_t, weight_refs, gated_ref, total_ref, column_ref):
-    atoms, channels = column_ref.shape
+def mix_block(b, kept_ref, weight_refs, gated_ref, beside):
+    channels = gated_ref.shape[0] // COMPONENTS
     lanes = gated_ref.shape[1]
     component_of = lambda degree, order: degree * degree + degree + order
     rows_of = lambda component: pl.ds(component * channels, channels)
@@ -477,6 +488,7 @@
         axis=0,
     )
     central = jnp.dot(weight_refs[0][...], gather(0), preferred_element_type=jnp.float32)
+    beside()
     gate = 1.0 / (1.0 + jnp.exp(-central[:channels]))
     for degree in range(DEGREES):
         gated_ref[rows_of(component_of(degree, 0)), :] = (
@@ -509,6 +521,11 @@
                     mixed[column * channels : (column + 1) * channels] * gate
                 ).astype(jnp.bfloat16)
 
+
+def sum_block(b, slots, frame_t, gated_ref, total_ref, column_ref):
+    atoms, channels = column_ref.shape
+    lanes = gated_ref.shape[1]
+    rows_of = lambda component: pl.ds(component * channels, channels)
     edge = iota((1, lanes), 1) + b * lanes
     home = edge // slots
     slot = edge - home * slots
@@ -597,6 +614,7 @@
             bf16(blocks, components, groups, height, lanes),
             bf16(narrow, wide * part, 128),
             bf16(components * channels, lanes),
+            bf16(components * channels, lanes),
             pltpu.VMEM((components, atoms, channels), jnp.float32),
             pltpu.VMEM((atoms, channels), jnp.float32),
             dma(len(stacks)),

time: 69.8 us -> 67.4 us (0.966)
  Pallas kernels: 67.5 us -> 65.1 us
    pallas_call x1, Pallas kernels: 67.5 us -> 65.1 us  [run(): pl.pallas_call(functools.partial(whole_kernel, (wide, narrow, len(stacks)...]
where the time goes in v5:
time: 67.4 us; the launch traced here: 67.2 us
  Pallas kernels  65.1 us (97%)
  local copies, waits for them, and re-layouts  2.12 us (3%)
    pallas_call x1, Pallas kernels, run(): pl.pallas_call(functools.partial(whole_kernel, (wide, narrow, len(stacks)...  65.1 us
    unnamed x1, local copies, waits for them, and re-layouts  2.12 us

profile of v5, /device:TPU:0, one launch (start us, length us, event | category | flops | bytes accessed | tf_op | source)
XLA Modules:
  0.0 67.2 jit_solution(6622231136015681338)
XLA Ops:
  0.0 65.1 %shard_map.109 = f32[25,64,128]{2,1,0:T(8,128)} custom-call(f32[4]{0:T(128)} %coefficient_ref.1, s32[48,64]{1,0:T(8,128)} %bitcast.18, s32[1,64]{1,0:T(1,128)} %bitcast.19, bf16[25,64,128]{2,1,0:T(8,128)(2,1)} %bitcast.16, bf16[3072,165]{1,0:T(8,128)(2,1)} %bitcast.13, bf16[3072,128]{1,0:T(8,128)(2,1)} %bitcast.15, bf16[4,640,640]{2,1,0:T(8,128)(2,1)} %refs_3_.1, ...), custom_call_target="tpu_custom_call" | custom-call | tf_op jit(solution)/shard_map/pallas_call | solution.py:590
  65.1 2.1 %copy.13 = f32[64,25,128]{2,0,1:T(8,128)} copy(f32[64,25,128]{2,0,1:T(8,128)} %bitcast.11) | data formatting | bytes 1638400

commit v6 on v5

--- a/solution.py
+++ b/solution.py
@@ -11,7 +11,7 @@
 DEGREES = 5
 COMPONENTS = DEGREES * DEGREES
 AXES = ("wide", "narrow")
-THREE = (1, 3)
+THREE = (1, 2, 3)
 MESH = pl.DeviceIdType.MESH
 EARLY = 2
 PLAN = (8, 10, 18, 22, 24, 28, 34, 38, 42, 48, 54)
@@ -499,15 +499,26 @@
         minus = gather(-order)
         if order in THREE:
             deep = plus.shape[0]
-            product = lambda at, right: jnp.dot(
-                weight_refs[order][:, at * deep : (at + 1) * deep],
-                right,
-                preferred_element_type=jnp.float32,
+            full = deep // 256 * 256
+            weight = weight_refs[order]
+            product = lambda left, right: jnp.dot(left, right, preferred_element_type=jnp.float32)
+            fully = lambda at, right: product(
+                weight[:, at * deep : at * deep + full], right[:full]
             )
-            both = product(0, plus + minus)
+            left_of = lambda at: weight[:, at * deep + full : (at + 1) * deep]
+            sums = plus + minus
+            both = fully(0, sums)
         for side in range(2):
             if order in THREE:
-                mixed = both - product(1, minus) if side == 0 else both + product(2, plus)
+                other = minus if side == 0 else plus
+                term = fully(side + 1, other)
+                mixed = both - term if side == 0 else both + term
+                if full < deep:
+                    tail = -other[full:] if side == 0 else other[full:]
+                    mixed = mixed + product(
+                        jnp.concatenate([left_of(0), left_of(side + 1)], axis=1),
+                        jnp.concatenate([sums[full:], tail], axis=0),
+                    )
             else:
                 pair = [plus, -minus] if side == 0 else [minus, plus]
                 mixed = jnp.dot(

time: 67.4 us -> 67.1 us (level)
  no operation moved by 1% of the time
where the time goes in v6:
time: 67.1 us; the launch traced here: 66.9 us
  Pallas kernels  64.8 us (97%)
  local copies, waits for them, and re-layouts  2.12 us (3%)
    pallas_call x1, Pallas kernels, run(): pl.pallas_call(functools.partial(whole_kernel, (wide, narrow, len(stacks)...  64.8 us
    unnamed x1, local copies, waits for them, and re-layouts  2.12 us

profile of v6, /device:TPU:0, one launch (start us, length us, event | category | flops | bytes accessed | tf_op | source)
XLA Modules:
  0.0 66.9 jit_solution(10466148125123825839)
XLA Ops:
  0.0 64.8 %shard_map.109 = f32[25,64,128]{2,1,0:T(8,128)} custom-call(f32[4]{0:T(128)} %coefficient_ref.1, s32[48,64]{1,0:T(8,128)} %bitcast.18, s32[1,64]{1,0:T(1,128)} %bitcast.19, bf16[25,64,128]{2,1,0:T(8,128)(2,1)} %bitcast.16, bf16[3072,165]{1,0:T(8,128)(2,1)} %bitcast.13, bf16[3072,128]{1,0:T(8,128)(2,1)} %bitcast.15, bf16[4,640,640]{2,1,0:T(8,128)(2,1)} %refs_3_.1, ...), custom_call_target="tpu_custom_call" | custom-call | tf_op jit(solution)/shard_map/pallas_call | solution.py:601
  64.8 2.1 %copy.13 = f32[64,25,128]{2,0,1:T(8,128)} copy(f32[64,25,128]{2,0,1:T(8,128)} %bitcast.11) | data formatting | bytes 1638400

commit v7 on v6

--- a/solution.py
+++ b/solution.py
@@ -14,7 +14,7 @@
 THREE = (1, 2, 3)
 MESH = pl.DeviceIdType.MESH
 EARLY = 2
-PLAN = (8, 10, 18, 22, 24, 28, 34, 38, 42, 48, 54)
+PLAN = (8, 10, 18, 22, 24, 26, 32, 36, 40, 44, 48)
 
 
 def flat_rows(weights):
@@ -210,7 +210,7 @@
         radial_t[b] = scales.reshape(radial_t.shape[1:])
         return carried
 
-    lax.fori_loop(0, blocks // 4, prepare, 0)
+    lax.fori_loop(0, blocks // 6, prepare, 0)
 
     pairing.wait_recv()
     scatter = []
@@ -231,7 +231,7 @@
             )
         )
         scatter[-1].start()
-    lax.fori_loop(blocks // 4, blocks, prepare, 0)
+    lax.fori_loop(blocks // 6, blocks, prepare, 0)
     mine = pl.ds(pl.multiple_of(my_core * half + my_chip * part, 16), part)
     there = pl.ds(pl.multiple_of(my_chip * part, 16), part)
     summed = partial_ref[mine, :].astype(jnp.float32) + paired_ref[there, :].astype(jnp.float32)

time: 67.1 us -> 67.1 us (level)
  no operation moved by 1% of the time
where the time goes in v7:
time: 67.1 us; the launch traced here: 66.9 us
  Pallas kernels  64.8 us (97%)
  local copies, waits for them, and re-layouts  2.12 us (3%)
    pallas_call x1, Pallas kernels, run(): pl.pallas_call(functools.partial(whole_kernel, (wide, narrow, len(stacks)...  64.8 us
    unnamed x1, local copies, waits for them, and re-layouts  2.12 us

profile of v7, /device:TPU:0, one launch (start us, length us, event | category | flops | bytes accessed | tf_op | source)
XLA Modules:
  0.0 66.9 jit_solution(9683221072849824269)
XLA Ops:
  0.0 64.8 %shard_map.109 = f32[25,64,128]{2,1,0:T(8,128)} custom-call(f32[4]{0:T(128)} %coefficient_ref.1, s32[48,64]{1,0:T(8,128)} %bitcast.18, s32[1,64]{1,0:T(1,128)} %bitcast.19, bf16[25,64,128]{2,1,0:T(8,128)(2,1)} %bitcast.16, bf16[3072,165]{1,0:T(8,128)(2,1)} %bitcast.13, bf16[3072,128]{1,0:T(8,128)(2,1)} %bitcast.15, bf16[4,640,640]{2,1,0:T(8,128)(2,1)} %refs_3_.1, ...), custom_call_target="tpu_custom_call" | custom-call | tf_op jit(solution)/shard_map/pallas_call | solution.py:601
  64.8 2.1 %copy.13 = f32[64,25,128]{2,0,1:T(8,128)} copy(f32[64,25,128]{2,0,1:T(8,128)} %bitcast.11) | data formatting | bytes 1638400
